TPU v7x, 128 devices: a whole 4x4x4 slice. The times are simulated.
128 devices in a mesh: seq: 32 (over y, z, core), batch: 4 (over x).
Axes of the slice: x: 4, y: 4, z: 4, core: 2. Of those that a mesh axis runs over, the one named last changes fastest.
Arguments:
- queries: bfloat16 [4, 4096, 4096], P('batch', 'seq'), may hold values from -130 to 130
- keys: bfloat16 [4, 4096, 1024], P('batch', 'seq'), may hold values from -4 to 4
- values: bfloat16 [4, 4096, 1024], P('batch', 'seq'), may hold values from -4 to 4
- lengths: int32 [4], P('batch'), may hold values from 2048 to 4096
- block_pos: int32 [4, 32], P('batch'), may hold values from 0 to 31, each once within a row
- w_in: bfloat16 [6144, 1024], replicated, may hold values from -0.078125 to 0.078125
- b_in: float32 [1024], replicated, may hold values from -3 to 3
- output_weight: bfloat16 [1024, 8], replicated, may hold values from -0.1875 to 0.1875
- output_bias: float32 [8], replicated, may hold values from 1 to 2
Outputs:
- grad_w_in: float32 [6144, 1024], P(('seq', 'batch'))
- grad_b_in: float32 [1024], replicated
- output_weight_gradient: float32 [1024, 8], replicated
- output_bias_gradient: float32 [8], replicated
Inputs may be any that keep to these rules, and one draw needn't show every extreme that they name: Each row of block_pos names every block 0 to 31 once.
All inputs are finite; a program needn't handle non-finite values.
Results may differ from a plain program's by a relative error of at most 0.0017.
The roundings to bfloat16 on the way count: a program that leaves them out, or rounds other values in their place, can miss the bound.
Values may be sent and summed in bfloat16 or wider, within the bound.
A program may use at most 128 MiB of HBM per device.

v0:
```python
import functools
import math

import jax
import jax.numpy as jnp
from jax import lax
from jax.experimental import pallas as pl
from jax.experimental.pallas import tpu as pltpu
from jax.sharding import PartitionSpec as P

F32 = jnp.float32
BF16 = jnp.bfloat16
PIECES = 2
MESH = pl.DeviceIdType.MESH


def copy_to(src, dst, send, recv, target):
    return pltpu.make_async_remote_copy(
        src_ref=src,
        dst_ref=dst,
        send_sem=send,
        recv_sem=recv,
        device_id=target,
        device_id_type=MESH,
    )


def kernel(
    n,
    nb,
    norm,
    scale,
    q_ref,
    k_ref,
    v_ref,
    w_ref,
    b_ref,
    wt_ref,
    bias_ref,
    order_ref,
    limit_ref,
    grad_ref,
    gb_ref,
    gw_ref,
    ob_ref,
    kg,
    ft,
    act,
    msum,
    mp,
    mr,
    delta,
    dg,
    otc,
    otr,
    obs,
    obr,
    ofin,
    dbs,
    dbr,
    cs,
    cr,
    ksem,
    fsem,
    msem,
    dsem,
    osem,
    bsem,
    gsem,
    hsem,
    csem,
    turned,
    weights_in,
    pre_ref,
    mask,
    ns,
    nr,
    nsem,
    wsem,
):
    me = lax.axis_index("seq")
    mb = lax.axis_index("batch")
    rows, kd = k_ref.shape
    heads = msum.shape[0]
    head = kd // heads
    per_group = q_ref.shape[1] // kd
    hidden = pre_ref.shape[1]
    load = pltpu.make_async_copy(w_ref, weights_in, wsem)
    load.start()
    inner = 2
    outer = n // inner
    mo = me // inner
    mi = me % inner
    pair = mo * inner + (inner - 1 - mi)

    def seq_peer(d):
        return lax.rem(me + d, n)

    def batch_peer(d):
        return lax.rem(mb + d, nb)

    def outer_peer(d):
        return lax.rem(mo + d, outer) * inner + mi

    def outer_source(d):
        return lax.rem(mo - d + outer, outer) * inner + mi

    barrier = pltpu.get_barrier_semaphore()
    for d in range(1, n):
        pl.semaphore_signal(barrier, inc=1, device_id={"seq": seq_peer(d)}, device_id_type=MESH)
    for d in range(1, nb):
        pl.semaphore_signal(
            barrier, inc=1, device_id={"batch": batch_peer(d)}, device_id_type=MESH
        )
    pl.semaphore_wait(barrier, n + nb - 2)

    def block(ref, owner):
        return ref.at[pl.ds(pl.multiple_of(owner * rows, rows), rows)]

    def gather_start(src, dst, sem):
        copies = []
        for d in range(1, outer):
            copy = copy_to(
                src, block(dst, me), sem.at[0, d], sem.at[1, d], {"seq": outer_peer(d)}
            )
            copy.start()
            copies.append(copy)
        copy = copy_to(src, block(dst, me), sem.at[2, 0], sem.at[3, 0], {"seq": pair})
        copy.start()
        return copies, [copy]

    def gather_finish(dst, sem, started):
        direct, passed = started
        for d in range(1, outer):
            direct[d - 1].wait_recv()
            held = block(dst, outer_source(d))
            copy = copy_to(held, held, sem.at[2, d], sem.at[3, d], {"seq": pair})
            copy.start()
            passed.append(copy)
        for copy in passed:
            copy.wait_recv()
        return direct + passed

    key_copies = gather_start(k_ref, kg, ksem)
    feat_copies = []
    cols = ft.shape[0]

    def send_features(first, last):
        for d in range(first, last):
            copy = copy_to(
                turned.at[pl.ds(pl.multiple_of(seq_peer(d) * cols, 16), cols)],
                ft.at[:, pl.ds(pl.multiple_of(me * rows, rows), rows)],
                fsem.at[0, d],
                fsem.at[1, d],
                {"seq": seq_peer(d)},
            )
            copy.start()
            feat_copies.append(copy)

    kg[pl.ds(pl.multiple_of(me * rows, rows), rows), :] = k_ref[...]
    base = 0
    for ref in (q_ref, k_ref, v_ref):

        def turn(c, carry, ref=ref, base=base):
            tile = ref[:, pl.ds(pl.multiple_of(c * head, head), head)]
            turned[pl.ds(pl.multiple_of(base + c * head, head), head), :] = tile.T
            return carry

        lax.fori_loop(0, ref.shape[1] // head, turn, 0)
        base += ref.shape[1]
    load.wait()
    tile_width = hidden // 4

    def project(c, carry):
        span = pl.ds(pl.multiple_of(c * tile_width, tile_width), tile_width)
        value = b_ref[:, span]
        base = 0
        for ref in (q_ref, k_ref, v_ref):
            depth = ref.shape[1]
            value = value + jnp.dot(
                ref[...], weights_in[base : base + depth, span], preferred_element_type=F32
            )
            base += depth
        pre_ref[:, span] = value
        act[:, span] = (value * jax.nn.sigmoid(value)).astype(BF16)
        return carry

    lax.fori_loop(0, 4, project, 0)
    ft[:, pl.ds(pl.multiple_of(me * rows, rows), rows)] = turned[
        pl.ds(pl.multiple_of(me * cols, 16), cols), :
    ]
    sent = gather_finish(kg, ksem, key_copies)
    early = n
    send_features(1, early)

    limit = limit_ref[0]
    lane = lax.broadcasted_iota(jnp.int32, (1, rows), 1)
    key_pos = jnp.concatenate([lane + order_ref[0, p] * rows for p in range(n)], axis=1)
    query_start = order_ref[0, me] * rows
    query_pos = lax.broadcasted_iota(jnp.int32, (rows, 1), 0) + query_start
    live_col = (query_pos < limit).astype(F32)
    live_row = (lane + query_start < limit).astype(F32)
    allowed = (key_pos <= query_pos) & (key_pos < limit)
    mask[...] = jnp.where(allowed, 0.0, -1e30)

    def group(g, carry):
        keys = kg[:, pl.ds(pl.multiple_of(g * head, head), head)]
        hide = mask[...]
        column = jnp.zeros((1, n * rows), F32)
        for j in range(per_group):
            start = pl.multiple_of((g * per_group + j) * head, head)
            score = lax.dot_general(
                q_ref[:, pl.ds(start, head)],
                keys,
                (((1,), (1,)), ((), ())),
                preferred_element_type=F32,
            )
            masked = jnp.where(hide < 0.0, hide, score * scale)
            top = jnp.max(masked, axis=1, keepdims=True)
            weights = jnp.exp(masked - top)
            denom = jnp.sum(weights, axis=1, keepdims=True)
            column += jnp.sum(weights * (live_col / denom), axis=0, keepdims=True)
        msum[g] = column
        return carry

    lax.fori_loop(0, heads, group, 0)
    for p in range(n):
        mp[p] = msum[:, 0, p * rows : (p + 1) * rows]
    mass_copies = []
    for d in range(1, n):
        copy = copy_to(
            mp.at[seq_peer(d)], mr.at[d], msem.at[0, d], msem.at[1, d], {"seq": seq_peer(d)}
        )
        copy.start()
        mass_copies.append(copy)
    wt = wt_ref[...]
    pred = (
        lax.dot_general(wt, act[...], (((1,), (1,)), ((), ())), preferred_element_type=F32)[:heads]
        + bias_ref[...]
    )
    mass = mp[me]
    for d in range(1, n):
        mass_copies[d - 1].wait_recv()
        mass = mass + mr[d]
    sent += mass_copies
    resid = ((pred - jnp.log1p(mass)) * live_row * norm).astype(BF16)
    resid32 = resid.astype(F32)
    resid_all = jnp.concatenate([resid32, jnp.zeros_like(resid32)], axis=0)
    resid_t = resid_all.T.astype(BF16)
    back = jnp.dot(resid_t, wt, preferred_element_type=F32)
    pre = pre_ref[...]
    sig = jax.nn.sigmoid(pre)
    slope = (back * sig * (1.0 + pre * (1.0 - sig))).astype(BF16)
    piece = hidden // PIECES
    delta_copies = []
    for h in range(PIECES):
        delta[h] = slope[:, h * piece : (h + 1) * piece]
        delta_copies.append(gather_start(delta.at[h], dg.at[h], dsem.at[h]))
        if h == 0:
            send_features(early, n)
        dg[h, pl.ds(pl.multiple_of(me * rows, rows), rows), :] = delta[h]

    out_term = jnp.dot(resid_all.astype(BF16), act[...], preferred_element_type=F32)
    width = hidden // n
    bias_sum = jnp.broadcast_to(jnp.sum(resid32, axis=1, keepdims=True), (heads, width))
    for p in range(n):
        otc[p, :heads] = out_term[:heads, p * width : (p + 1) * width]
        otc[p, heads:] = bias_sum
    first = []
    for d in range(1, n):
        copy = copy_to(
            otc.at[seq_peer(d)], otr.at[d], osem.at[0, d], osem.at[1, d], {"seq": seq_peer(d)}
        )
        copy.start()
        first.append(copy)
    small = otc[me]
    for d in range(1, n):
        first[d - 1].wait_recv()
        small = small + otr[d]
    obs[...] = small
    second = []
    for d in range(1, nb):
        copy = copy_to(
            obs, obr.at[d], bsem.at[0, d], bsem.at[1, d], {"batch": batch_peer(d)}
        )
        copy.start()
        second.append(copy)

    part = cr.shape[2]
    bo = mb // inner
    bi = mb % inner
    bouter = nb // inner
    twin = bo * inner + (inner - 1 - bi)

    def term(h, owner):
        start = pl.multiple_of(owner * part, 16)
        return jnp.dot(ft[pl.ds(start, part), :], dg[h], preferred_element_type=F32)

    chunks = []
    near = []
    for h in range(PIECES):
        sent += gather_finish(dg.at[h], dsem.at[h], delta_copies[h])
        if h == 0:
            for copy in feat_copies:
                copy.wait_recv()
        swaps = []
        for e in range(bouter):
            ahead = lax.rem(bo + 1 + e, bouter)
            ns[h, e] = term(h, ahead * inner + (inner - 1 - bi))
            copy = copy_to(
                ns.at[h, e], nr.at[h, e], nsem.at[0, h, e], nsem.at[1, h, e], {"batch": twin}
            )
            copy.start()
            swaps.append(copy)
        near += swaps
        for e in range(bouter):
            ahead = lax.rem(bo + 1 + e, bouter)
            value = term(h, ahead * inner + bi)
            swaps[e].wait_recv()
            value = value + nr[h, e]
            if e == bouter - 1:
                grad_ref[:, h * piece : (h + 1) * piece] = value
            else:
                cs[h, e] = value
                copy = copy_to(
                    cs.at[h, e],
                    cr.at[h, e],
                    csem.at[0, h, e],
                    csem.at[1, h, e],
                    {"batch": ahead * inner + bi},
                )
                copy.start()
                chunks.append((h, e, copy))
        dbs[:, h * piece : (h + 1) * piece] = jnp.dot(
            jnp.ones((8, n * rows), BF16), dg[h], preferred_element_type=F32
        )
    sums = []
    for d in range(1, nb):
        copy = copy_to(
            dbs, dbr.at[d], gsem.at[0, d], gsem.at[1, d], {"batch": batch_peer(d)}
        )
        copy.start()
        sums.append(copy)

    small = obs[...]
    for d in range(1, nb):
        second[d - 1].wait_recv()
        small = small + obr[d]
    ofin[me] = small
    third = []
    for d in range(1, n):
        copy = copy_to(
            ofin.at[me], ofin.at[me], hsem.at[0, d], hsem.at[1, d], {"seq": seq_peer(d)}
        )
        copy.start()
        third.append(copy)
    for h, e, copy in chunks:
        copy.wait_recv()
        grad_ref[:, h * piece : (h + 1) * piece] += cr[h, e]
    grad_b = dbs[...]
    for d in range(1, nb):
        sums[d - 1].wait_recv()
        grad_b = grad_b + dbr[d]
    gb_ref[...] = grad_b[:1]
    for copy in third:
        copy.wait_recv()
    gw_ref[...] = jnp.concatenate([ofin[p, :heads] for p in range(n)], axis=1).T
    ob_ref[...] = ofin[0, heads:, :1]
    for copy in sent + feat_copies + first + second + near + sums + third + [c[2] for c in chunks]:
        copy.wait_send()


def on_device(queries, keys, values, lengths, block_pos, w_in, b_in, output_weight, output_bias):
    n = lax.axis_size("seq")
    nb = lax.axis_size("batch")
    q_rows = queries[0]
    k_rows = keys[0]
    v_rows = values[0]
    rows, kd = k_rows.shape
    heads = output_weight.shape[1]
    hidden = w_in.shape[1]
    feat = w_in.shape[0]
    cols = feat // n
    part = cols // nb
    scale = 1.0 / math.sqrt(kd // heads)
    norm = 1.0 / math.sqrt(nb * n * rows)
    wt = jnp.pad(output_weight.T, ((0, heads), (0, 0)))
    vmem = pl.BlockSpec(memory_space=pltpu.VMEM)
    total = n * rows
    width = hidden // n
    grad, gb, gw, ob = pl.pallas_call(
        functools.partial(kernel, n, nb, norm, scale),
        out_shape=(
            jax.ShapeDtypeStruct((part, hidden), F32),
            jax.ShapeDtypeStruct((1, hidden), F32),
            jax.ShapeDtypeStruct((hidden, heads), F32),
            jax.ShapeDtypeStruct((heads, 1), F32),
        ),
        in_specs=[vmem] * 3
        + [pl.BlockSpec(memory_space=pl.ANY)]
        + [vmem] * 3
        + [pl.BlockSpec(memory_space=pltpu.SMEM)] * 2,
        out_specs=(vmem, vmem, vmem, vmem),
        scratch_shapes=[
            pltpu.VMEM((total, kd), BF16),
            pltpu.VMEM((cols, total), BF16),
            pltpu.VMEM((rows, hidden), BF16),
            pltpu.VMEM((heads, 1, total), F32),
            pltpu.VMEM((n, heads, rows), F32),
            pltpu.VMEM((n, heads, rows), F32),
            pltpu.VMEM((PIECES, rows, hidden // PIECES), BF16),
            pltpu.VMEM((PIECES, total, hidden // PIECES), BF16),
            pltpu.VMEM((n, 2 * heads, width), F32),
            pltpu.VMEM((n, 2 * heads, width), F32),
            pltpu.VMEM((2 * heads, width), F32),
            pltpu.VMEM((nb, 2 * heads, width), F32),
            pltpu.VMEM((n, 2 * heads, width), F32),
            pltpu.VMEM((8, hidden), F32),
            pltpu.VMEM((nb, 8, hidden), F32),
            pltpu.VMEM((PIECES, nb // 2, part, hidden // PIECES), F32),
            pltpu.VMEM((PIECES, nb // 2, part, hidden // PIECES), F32),
            pltpu.SemaphoreType.DMA((4, n)),
            pltpu.SemaphoreType.DMA((2, n)),
            pltpu.SemaphoreType.DMA((2, n)),
            pltpu.SemaphoreType.DMA((PIECES, 4, n)),
            pltpu.SemaphoreType.DMA((2, n)),
            pltpu.SemaphoreType.DMA((2, nb)),
            pltpu.SemaphoreType.DMA((2, nb)),
            pltpu.SemaphoreType.DMA((2, n)),
            pltpu.SemaphoreType.DMA((2, PIECES, nb)),
            pltpu.VMEM((feat, rows), BF16),
            pltpu.VMEM((feat, hidden), BF16),
            pltpu.VMEM((rows, hidden), F32),
            pltpu.VMEM((rows, total), F32),
            pltpu.VMEM((PIECES, nb // 2, part, hidden // PIECES), F32),
            pltpu.VMEM((PIECES, nb // 2, part, hidden // PIECES), F32),
            pltpu.SemaphoreType.DMA((2, PIECES, nb)),
            pltpu.SemaphoreType.DMA,
        ],
        compiler_params=pltpu.CompilerParams(
            collective_id=0, has_side_effects=True, vmem_limit_bytes=60 * 1024 * 1024
        ),
    )(
        q_rows,
        k_rows,
        v_rows,
        w_in,
        b_in[None, :],
        wt,
        output_bias[:, None],
        block_pos,
        lengths,
    )
    return (grad, gb[0], gw, ob[:, 0])


def solution(mesh):
    return jax.shard_map(
        on_device,
        mesh=mesh,
        in_specs=(
            P("batch", "seq", None),
            P("batch", "seq", None),
            P("batch", "seq", None),
            P("batch"),
            P("batch", None),
            P(),
            P(),
            P(),
            P(),
        ),
        out_specs=(P(("seq", "batch"), None), P(), P(), P()),
        check_vma=False,
    )
```

profile of v0, /device:TPU:8, one launch (start us, length us, event | category | flops | bytes accessed | tf_op | source)
XLA Modules:
  0.0 265.1 jit_solution(15202944154864477073)
XLA Ops:
  1.3 1.3 copy.15.bias_ref
  2.6 1.3 pad.4.wt_ref
  3.9 255.1 %shard_map.120 = (f32[48,1024]{1,0:T(8,128)}, f32[1,1024]{1,0:T(1,128)}, f32[1024,8]{1,0:T(8,128)}, f32[8,1]{1,0:T(8,128)}) custom-call(bf16[128,4096]{1,0:T(8,128)(2,1)} %bitcast.7, bf16[128,1024]{1,0:T(8,128)(2,1)} %bitcast.8, bf16[128,1024]{1,0:T(8,128)(2,1)} %bitcast.9, bf16[6144,1024]{1,0:T(8,128)(2,1)} %w_ref.1, f32[1,1024]{1,0:T(1,128)} %bitcast.11, ...), custom_call_target="tpu_custom_call" | custom-call | tf_op jit(solution)/shard_map/pallas_call | solution.py:391
  259.0 1.3 reduce
  260.3 1.8 copy.16
  262.2 1.6 copy.20
  263.8 1.3 copy.21
where the time goes:
time: 269 us; the launch traced here: 265 us
  Pallas kernels  255 us (95%)
  local copies, waits for them, and re-layouts  7.37 us (3%)
    pallas_call x1, Pallas kernels, on_device(): pl.pallas_call(functools.partial(kernel, n, nb, norm, scale), out_shape=(...  255 us

commit v1 on v0

v1 whole, which is shorter than its diff:
```python
import functools
import math

import jax
import jax.numpy as jnp
from jax import lax
from jax.experimental import pallas as pl
from jax.experimental.pallas import tpu as pltpu
from jax.sharding import PartitionSpec as P

F32 = jnp.float32
BF16 = jnp.bfloat16
MESH = pl.DeviceIdType.MESH
SIDE = 4
ROUNDS = 2
GRAN = 16
LOG2E = 1.4426950408889634


def copy_to(src, dst, sems, index, target):
    return pltpu.make_async_remote_copy(
        src_ref=src,
        dst_ref=dst,
        send_sem=sems.at[(0, *index)],
        recv_sem=sems.at[(1, *index)],
        device_id=target,
        device_id_type=MESH,
    )


def kernel(
    n,
    nb,
    norm,
    scale,
    q_ref,
    k_ref,
    v_ref,
    w_ref,
    b_ref,
    wt_ref,
    bias_ref,
    order_ref,
    inv_ref,
    limit_ref,
    grad_ref,
    gb_ref,
    gw_ref,
    ob_ref,
    win,
    qg,
    kg,
    ks,
    qo,
    kt,
    ft,
    vt,
    slope,
    act,
    sref,
    colacc,
    mp,
    mr,
    dg,
    otc,
    otr,
    obs,
    obr,
    ofin,
    cs,
    cr,
    sb,
    xr,
    fin,
    fout,
    wsem,
    qsem,
    ksem,
    kpsem,
    qpsem,
    vsem,
    msem,
    asem,
    osem,
    bsem,
    hsem,
    psem,
    xsem,
    gsem,
):
    me = lax.axis_index("seq")
    mb = lax.axis_index("batch")
    rows, kd = k_ref.shape
    hidden = slope.shape[1]
    heads = wt_ref.shape[0] // 2
    head = kd // heads
    chips = n // 2
    chip = me // 2
    core = me % 2
    pair = chip * 2 + (1 - core)
    cy = chip // SIDE
    cz = chip % SIDE
    load = pltpu.make_async_copy(w_ref, win, wsem)
    load.start()

    def seq_peer(d):
        return lax.rem(me + d, n)

    def chip_peer(d):
        return lax.rem(chip + d, chips)

    def chip_source(d):
        return lax.rem(chip - d + chips, chips)

    def batch_peer(d):
        return lax.rem(mb + d, nb)

    def at(i, size):
        return pl.ds(pl.multiple_of(i * size, size), size)

    barrier = pltpu.get_barrier_semaphore()
    for d in range(1, n):
        pl.semaphore_signal(barrier, inc=1, device_id={"seq": seq_peer(d)}, device_id_type=MESH)
    for d in range(1, nb):
        pl.semaphore_signal(
            barrier, inc=1, device_id={"batch": batch_peer(d)}, device_id_type=MESH
        )

    def turn_values(j, carry):
        vt[at(j, head), :] = v_ref[:, at(j, head)].T
        return carry

    lax.fori_loop(0, kd // head, turn_values, 0)
    pl.semaphore_wait(barrier, n + nb - 2)

    key_far = []
    for d in range(1, chips):
        to = chip_peer(d)
        copy = copy_to(
            k_ref.at[:, at(to // 2, head)], kg.at[me], ksem, (d,), {"seq": to * 2 + core}
        )
        copy.start()
        key_far.append(copy)
    key_near = [
        copy_to(k_ref.at[:, at(chip // 2, head)], kg.at[me], kpsem, (0,), {"seq": pair})
    ]
    key_near[0].start()
    queries_sent = []
    for d in range(1, n):
        to = seq_peer(d)
        copy = copy_to(
            q_ref.at[:, at(to, head)], qg.at[me], qsem, (d,), {"seq": to}
        )
        copy.start()
        queries_sent.append(copy)
    vpart = kd // chips
    value_base = 2 * head + vpart
    values_sent = []
    for d in range(1, chips):
        to = chip_peer(d)
        copy = copy_to(
            vt.at[at(to, vpart)],
            ft.at[pl.ds(value_base, vpart), at(chip, rows)],
            vsem,
            (d,),
            {"seq": to * 2 + core},
        )
        copy.start()
        values_sent.append(copy)
    qg[me] = q_ref[:, at(me, head)]
    qo[at(chip, rows), :] = q_ref[:, at(pair, head)]
    kg[me] = k_ref[:, at(chip // 2, head)]
    ft[pl.ds(value_base, vpart), at(chip, rows)] = vt[at(chip, vpart), :]

    load.wait()
    tile = hidden // 4

    def project(j, carry):
        span = at(j, tile)
        value = b_ref[:, span]
        base = 0
        for ref in (q_ref, k_ref, v_ref):
            depth = ref.shape[1]
            value = value + jnp.dot(
                ref[...], win[base : base + depth, span], preferred_element_type=F32
            )
            base += depth
        sig = jax.nn.sigmoid(value)
        slope[:, span] = sig * (1.0 + value * (1.0 - sig))
        act[:, span] = (value * sig).astype(BF16)
        return carry

    lax.fori_loop(0, 4, project, 0)
    wt = wt_ref[...]
    pred = (
        lax.dot_general(wt, act[...], (((1,), (1,)), ((), ())), preferred_element_type=F32)[:heads]
        + bias_ref[...]
    )

    for d in range(1, chips):
        key_far[d - 1].wait_recv()
        held = kg.at[chip_source(d) * 2 + core]
        copy = copy_to(held, held, kpsem, (d,), {"seq": pair})
        copy.start()
        key_near.append(copy)
    for d in range(1, n):
        queries_sent[d - 1].wait_recv()
    queries_passed = []
    for d in range(1, chips):
        source = chip_source(d)
        copy = copy_to(
            qg.at[source * 2 + (1 - core)],
            qo.at[at(source, rows)],
            qpsem,
            (d,),
            {"seq": pair},
        )
        copy.start()
        queries_passed.append(copy)
    for copy in key_near:
        copy.wait_recv()

    limit = limit_ref[0]

    def sort_keys(p, carry):
        ks[at(p, rows), :] = kg[inv_ref[0, p]]
        return carry

    lax.fori_loop(0, n, sort_keys, 0)
    colacc[...] = jnp.zeros_like(colacc)
    step = 4
    wide = step * rows
    row_index = lax.broadcasted_iota(jnp.int32, (rows, 1), 0)
    lane_wide = lax.broadcasted_iota(jnp.int32, (1, wide), 1)

    for w in range(n // step):

        def query_block(t, carry, w=w):
            block = w * step + t
            queries = qg[inv_ref[0, block]]
            best = None
            for kc in range(w + 1):
                score = lax.dot_general(
                    queries,
                    ks[kc * wide : (kc + 1) * wide, :],
                    (((1,), (1,)), ((), ())),
                    preferred_element_type=F32,
                )
                if kc == w:
                    score = jnp.where(lane_wide <= row_index + t * rows, score, -1e30)
                sref[:, kc * wide : (kc + 1) * wide] = score
                for j in range(step):
                    part = score[:, j * rows : (j + 1) * rows]
                    best = part if best is None else jnp.maximum(best, part)
            top = jnp.max(best, axis=1, keepdims=True)
            total = None
            for kb in range((w + 1) * step):
                span = slice(kb * rows, (kb + 1) * rows)
                weight = jnp.exp2((sref[:, span] - top) * (scale * LOG2E))
                sref[:, span] = weight
                total = weight if total is None else total + weight
            denom = jnp.sum(total, axis=1, keepdims=True)
            live = (row_index + block * rows < limit).astype(F32)
            share = live / denom
            for kb in range((w + 1) * step):
                span = slice(kb * rows, (kb + 1) * rows)
                part = sref[:, span] * share
                colacc[kb] += jnp.sum(part.reshape(rows // 8, 8, rows), axis=0)
            return carry

        lax.fori_loop(0, step, query_block, 0)

    for t in range(n):
        mp[t] = colacc[order_ref[0, t]]
    mass_sent = []
    for d in range(1, n):
        to = seq_peer(d)
        copy = copy_to(mp.at[to], mr.at[me], msem, (d,), {"seq": to})
        copy.start()
        mass_sent.append(copy)
    mr[me] = mp[me]

    for copy in queries_passed:
        copy.wait_recv()
    for copy in values_sent:
        copy.wait_recv()

    def turn_features(s, carry):
        ft[at(core, head), at(s, rows)] = qg[2 * s + core].T
        ft[at(1 - core, head), at(s, rows)] = qo[at(s, rows), :].T
        kt[:, at(s, rows)] = kg[2 * s + core].T
        return carry

    lax.fori_loop(0, chips, turn_features, 0)
    ft[pl.ds(2 * head, vpart), :] = kt[at(chip % 2, vpart), :]

    for copy in mass_sent:
        copy.wait_recv()
    per_group = n // heads
    sums = []
    for g in range(heads):
        value = mr[g * per_group]
        for j in range(1, per_group):
            value = value + mr[g * per_group + j]
        sums.append(jnp.sum(value, axis=0, keepdims=True))
    mass = jnp.concatenate(sums, axis=0)
    lane = lax.broadcasted_iota(jnp.int32, (1, rows), 1)
    live_row = (lane + order_ref[0, me] * rows < limit).astype(F32)
    resid = ((pred - jnp.log1p(mass)) * live_row * norm).astype(BF16)
    resid32 = resid.astype(F32)
    resid_all = jnp.concatenate([resid32, jnp.zeros_like(resid32)], axis=0)
    back = jnp.dot(resid_all.T.astype(BF16), wt, preferred_element_type=F32)
    delta = (back * slope[...]).astype(BF16)
    blocks = hidden // rows
    for j in range(blocks):
        dg[j, at(chip, rows), :] = delta[:, j * rows : (j + 1) * rows]

    classes = blocks // ROUNDS
    gathered = {}

    def place(k, a, b):
        dy, dz = (a, b) if k < 2 else (b, a)
        return lax.rem(cy + SIDE - dy, SIDE) * SIDE + lax.rem(cz + SIDE - dz, SIDE)

    def forward(r, k, a, b, axis, move):
        along_y = (axis == 0) == (k < 2)
        if along_y:
            to = lax.rem(cy + SIDE + move, SIDE) * SIDE + cz
        else:
            to = cy * SIDE + lax.rem(cz + SIDE + move, SIDE)
        a2, b2 = ((a + move) % SIDE, b) if axis == 0 else (a, (b + move) % SIDE)
        part = dg.at[r * classes + k, at(place(k, a, b), rows)]
        copy = copy_to(part, part, asem, (r, k, a2 * SIDE + b2), {"seq": to * 2 + core})
        copy.start()
        gathered[r, k, a2, b2] = copy

    def arrive(r, k, a, b):
        gathered[r, k, a, b].wait_recv()

    def toward(k):
        return (1, 1, 3) if k % 2 == 0 else (-1, 3, 1)

    def stage0(r):
        for k in range(classes):
            for axis in (0, 1):
                for move in (1, -1):
                    forward(r, k, 0, 0, axis, move)

    def stage1(r):
        for k in range(classes):
            move, near, far = toward(k)
            arrive(r, k, near, 0)
            forward(r, k, near, 0, 0, move)
            forward(r, k, near, 0, 1, 1)
            forward(r, k, near, 0, 1, -1)
        for k in range(classes):
            move, near, far = toward(k)
            arrive(r, k, far, 0)
            forward(r, k, far, 0, 1, 1)
            forward(r, k, far, 0, 1, -1)

    def stage2(r):
        for k in range(classes):
            move, near, far = toward(k)
            arrive(r, k, 0, near)
            forward(r, k, 0, near, 1, move)
        for k in range(classes):
            arrive(r, k, 2, 0)
            forward(r, k, 2, 0, 1, 1)
            forward(r, k, 2, 0, 1, -1)

    def stage3(r):
        for a in (0, 1):
            for k in range(classes):
                move, near, far = toward(k)
                line = near if a == 0 else far
                arrive(r, k, line, near)
                forward(r, k, line, near, 1, move)

    def stage4(r):
        for k in range(classes):
            move, near, far = toward(k)
            arrive(r, k, 2, near)
            forward(r, k, 2, near, 1, move)

    def stage5(r):
        for k in range(classes):
            move, near, far = toward(k)
            for a in range(SIDE):
                arrive(r, k, a, far)
                arrive(r, k, a, 2)

    stage0(0)
    out_term = jnp.dot(resid_all.astype(BF16), act[...], preferred_element_type=F32)
    width = hidden // n
    bias_sum = jnp.broadcast_to(jnp.sum(resid32, axis=1, keepdims=True), (heads, width))
    delta_sum = jnp.sum(delta.astype(F32), axis=0, keepdims=True)
    for p in range(n):
        otc[p, :heads] = out_term[:heads, p * width : (p + 1) * width]
        otc[p, heads : 2 * heads] = bias_sum
        otc[p, 2 * heads :] = jnp.broadcast_to(
            delta_sum[:, p * width : (p + 1) * width], (heads, width)
        )
    stage1(0)
    stage0(1)
    first = []
    for d in range(1, n):
        to = seq_peer(d)
        copy = copy_to(otc.at[to], otr.at[d], osem, (d,), {"seq": to})
        copy.start()
        first.append(copy)
    stage2(0)
    stage3(0)
    stage1(1)
    small = otc[me]
    for d in range(1, n):
        first[d - 1].wait_recv()
        small = small + otr[d]
    obs[...] = small
    second = []
    for d in range(1, nb):
        copy = copy_to(obs, obr.at[d], bsem, (d,), {"batch": batch_peer(d)})
        copy.start()
        second.append(copy)
    stage4(0)
    stage2(1)
    stage5(0)

    half = ft.shape[0] // 2
    piece = hidden // ROUNDS
    share_rows = half // GRAN // nb

    def term(r, which):
        lhs = ft[at(which, half), :]
        parts = []
        for j in range(0, classes, 2):
            rhs = jnp.concatenate([dg[r * classes + j], dg[r * classes + j + 1]], axis=1)
            parts.append(jnp.dot(lhs, rhs, preferred_element_type=F32))
        return jnp.concatenate(parts, axis=1)

    def start_of(target):
        return lax.rem(share_rows * target + 2 * SIDE * chip, half // GRAN)

    swaps = []
    spread = []

    def swap(r):
        cs[r] = term(r, 1 - core)
        copy = copy_to(cs.at[r], cr.at[r], psem, (r,), {"seq": pair})
        copy.start()
        swaps.append(copy)

    def reduce_chip(r):
        own = term(r, core)
        swaps[r].wait_recv()
        both = (own + cr[r]).reshape(half // GRAN, GRAN, piece)
        sb[r, : half // GRAN] = both
        sb[r, half // GRAN :] = both[: share_rows - 1]
        for d in (2, 1, 3):
            to = batch_peer(d)
            copy = copy_to(
                sb.at[r, pl.ds(start_of(to), share_rows)],
                xr.at[r, d],
                xsem,
                (r, d),
                {"batch": to},
            )
            copy.start()
            spread.append((r, copy))

    def granule(i):
        q_gran = 2 * head // GRAN
        k_gran = vpart // GRAN
        total_q = n * head // GRAN
        total_k = kd // GRAN
        return jnp.where(
            i < q_gran,
            q_gran * chip + i,
            jnp.where(
                i < q_gran + k_gran,
                total_q + k_gran * chip + i - q_gran,
                total_q + total_k + k_gran * chip + i - q_gran - k_gran,
            ),
        )

    per_dev = share_rows * nb

    def owner_of(e):
        o = lax.rem(start_of(mb) + e, half // GRAN)
        return granule(o + core * (half // GRAN)) // per_dev

    def maker_of(e):
        q_gran = 2 * head // GRAN
        k_gran = vpart // GRAN
        total_q = n * head // GRAN
        total_k = kd // GRAN
        u = per_dev * me + share_rows * mb + e
        uk = u - total_q
        uv = uk - total_k
        which = jnp.where(
            uk < 0, u // q_gran, jnp.where(uv < 0, uk // k_gran, uv // k_gran)
        )
        i = jnp.where(
            uk < 0,
            u % q_gran,
            jnp.where(uv < 0, q_gran + uk % k_gran, q_gran + k_gran + uv % k_gran),
        )
        return which * 2 + jnp.where(i >= half // GRAN, 1, 0)

    def final_copy(r, e):
        return copy_to(fin.at[r, e], fout.at[r, e], gsem, (r, e), {"seq": owner_of(e)})

    def finish(r):
        value = sb[r, pl.ds(start_of(mb), share_rows)]
        for which, copy in spread:
            if which == r:
                copy.wait_recv()
        for d in range(1, nb):
            value = value + xr[r, d]
        fin[r] = value
        for e in range(share_rows):
            stays = owner_of(e) == me

            @pl.when(jnp.logical_not(stays))
            def _(r=r, e=e):
                final_copy(r, e).start()

            @pl.when(stays)
            def _(r=r, e=e):
                fout[r, e] = fin[r, e]

    swap(0)
    stage3(1)
    reduce_chip(0)
    stage4(1)
    small = obs[...]
    for d in range(1, nb):
        second[d - 1].wait_recv()
        small = small + obr[d]
    ofin[me] = small
    third = []
    for d in range(1, n):
        copy = copy_to(ofin.at[me], ofin.at[me], hsem, (d,), {"seq": seq_peer(d)})
        copy.start()
        third.append(copy)
    stage5(1)
    swap(1)
    finish(0)
    reduce_chip(1)
    for copy in third:
        copy.wait_recv()
    gw_ref[...] = jnp.concatenate([ofin[p, :heads] for p in range(n)], axis=1).T
    ob_ref[...] = ofin[0, heads : 2 * heads, :1]
    gb_ref[...] = jnp.concatenate([ofin[p, 2 * heads : 2 * heads + 1] for p in range(n)], axis=1)
    finish(1)
    for r in range(ROUNDS):
        for e in range(share_rows):

            @pl.when(maker_of(e) != me)
            def _(r=r, e=e):
                final_copy(r, e).wait_recv()

            grad_ref[e * GRAN : (e + 1) * GRAN, r * piece : (r + 1) * piece] = fout[r, e]
    for copy in (
        key_far
        + key_near
        + queries_sent
        + queries_passed
        + values_sent
        + mass_sent
        + list(gathered.values())
        + first
        + second
        + third
        + swaps
        + [copy for _, copy in spread]
    ):
        copy.wait_send()
    for r in range(ROUNDS):
        for e in range(share_rows):

            @pl.when(owner_of(e) != me)
            def _(r=r, e=e):
                final_copy(r, e).wait_send()


def on_device(queries, keys, values, lengths, block_pos, w_in, b_in, output_weight, output_bias):
    n = lax.axis_size("seq")
    nb = lax.axis_size("batch")
    q_rows = queries[0]
    k_rows = keys[0]
    v_rows = values[0]
    rows, kd = k_rows.shape
    heads = output_weight.shape[1]
    hidden = w_in.shape[1]
    feat = w_in.shape[0]
    head = kd // heads
    scale = 1.0 / math.sqrt(head)
    norm = 1.0 / math.sqrt(nb * n * rows)
    wt = jnp.pad(output_weight.T, ((0, heads), (0, 0)))
    vmem = pl.BlockSpec(memory_space=pltpu.VMEM)
    total = n * rows
    chips = n // 2
    part = feat // n // nb
    width = hidden // n
    chip_feat = feat // chips
    piece = hidden // ROUNDS
    grans = chip_feat // 2 // GRAN
    share_rows = grans // nb
    places = jnp.arange(n, dtype=jnp.int32)
    inverse = jnp.sum(
        jnp.where(block_pos[0][None, :] == places[:, None], places[None, :], 0), axis=1
    )[None, :]
    dma = pltpu.SemaphoreType.DMA
    grad, gb, gw, ob = pl.pallas_call(
        functools.partial(kernel, n, nb, norm, scale),
        out_shape=(
            jax.ShapeDtypeStruct((part, hidden), F32),
            jax.ShapeDtypeStruct((1, hidden), F32),
            jax.ShapeDtypeStruct((hidden, heads), F32),
            jax.ShapeDtypeStruct((heads, 1), F32),
        ),
        in_specs=[vmem] * 3
        + [pl.BlockSpec(memory_space=pl.ANY)]
        + [vmem] * 3
        + [pl.BlockSpec(memory_space=pltpu.SMEM)] * 3,
        out_specs=(vmem, vmem, vmem, vmem),
        scratch_shapes=[
            pltpu.VMEM((feat, hidden), BF16),
            pltpu.VMEM((n, rows, head), BF16),
            pltpu.VMEM((n, rows, head), BF16),
            pltpu.VMEM((total, head), BF16),
            pltpu.VMEM((total // 2, head), BF16),
            pltpu.VMEM((head, total // 2), BF16),
            pltpu.VMEM((chip_feat, total // 2), BF16),
            pltpu.VMEM((kd, rows), BF16),
            pltpu.VMEM((rows, hidden), F32),
            pltpu.VMEM((rows, hidden), BF16),
            pltpu.VMEM((rows, total), F32),
            pltpu.VMEM((n, 8, rows), F32),
            pltpu.VMEM((n, 8, rows), F32),
            pltpu.VMEM((n, 8, rows), F32),
            pltpu.VMEM((hidden // rows, total // 2, rows), BF16),
            pltpu.VMEM((n, 3 * heads, width), F32),
            pltpu.VMEM((n, 3 * heads, width), F32),
            pltpu.VMEM((3 * heads, width), F32),
            pltpu.VMEM((nb, 3 * heads, width), F32),
            pltpu.VMEM((n, 3 * heads, width), F32),
            pltpu.VMEM((ROUNDS, chip_feat // 2, piece), F32),
            pltpu.VMEM((ROUNDS, chip_feat // 2, piece), F32),
            pltpu.VMEM((ROUNDS, grans + share_rows - 1, GRAN, piece), F32),
            pltpu.VMEM((ROUNDS, nb, share_rows, GRAN, piece), F32),
            pltpu.VMEM((ROUNDS, share_rows, GRAN, piece), F32),
            pltpu.VMEM((ROUNDS, share_rows, GRAN, piece), F32),
            dma,
            dma((2, n)),
            dma((2, chips)),
            dma((2, chips)),
            dma((2, chips)),
            dma((2, chips)),
            dma((2, n)),
            dma((2, ROUNDS, hidden // rows // ROUNDS, SIDE * SIDE)),
            dma((2, n)),
            dma((2, nb)),
            dma((2, n)),
            dma((2, ROUNDS)),
            dma((2, ROUNDS, nb)),
            dma((2, ROUNDS, share_rows)),
        ],
        compiler_params=pltpu.CompilerParams(
            collective_id=0, has_side_effects=True, vmem_limit_bytes=60 * 1024 * 1024
        ),
    )(
        q_rows,
        k_rows,
        v_rows,
        w_in,
        b_in[None, :],
        wt,
        output_bias[:, None],
        block_pos,
        inverse,
        lengths,
    )
    return (grad, gb[0], gw, ob[:, 0])


def solution(mesh):
    return jax.shard_map(
        on_device,
        mesh=mesh,
        in_specs=(
            P("batch", "seq", None),
            P("batch", "seq", None),
            P("batch", "seq", None),
            P("batch"),
            P("batch", None),
            P(),
            P(),
            P(),
            P(),
        ),
        out_specs=(P(("seq", "batch"), None), P(), P(), P()),
        check_vma=False,
    )
```

time: 269 us -> 126 us (0.47); the launches traced: 265 us -> 125 us
  Pallas kernels: 255 us -> 114 us
    pallas_call x1, Pallas kernels: 255 us -> 114 us  [on_device(): pl.pallas_call(functools.partial(kernel, n, nb, norm, scale), out_shape=(...]
where the time goes in v1:
time: 126 us; the launch traced here: 125 us
  Pallas kernels  114 us (90%)
  local copies, waits for them, and re-layouts  7.37 us (6%)
  other arithmetic  2.6 us (2%)
  between operations  1.29 us (1%)
    pallas_call x1, Pallas kernels, on_device(): pl.pallas_call(functools.partial(kernel, n, nb, norm, scale), out_shape=(...  114 us
    unnamed x3, local copies, waits for them, and re-layouts  4.71 us

profile of v1, /device:TPU:8, one launch (start us, length us, event | category | flops | bytes accessed | tf_op | source)
XLA Modules:
  0.0 125.0 jit_solution(14902981278513289118)
XLA Ops:
  1.3 1.3 %select_reduce_fusion = s32[32]{0:T(128)} fusion(s32[32]{0:T(128)} %bitcast.15), kind=kLoop, calls=%fused_computation | loop fusion | flops 3040 | bytes 256 | tf_op jit(solution)/shard_map/reduce_sum | solution.py:611
  2.6 1.3 %copy.17.bias_ref = f32[8,1]{1,0:T(8,128)} copy(f32[8,1]{0,1:T(1,128)} %bitcast.17) | data formatting | bytes 64 | tf_op jit(solution)/shard_map/broadcast_in_dim | solution.py:680
  3.9 1.3 %pad.4.wt_ref = bf16[16,1024]{1,0:T(8,128)(2,1)} pad(bf16[8,1024]{1,0:T(8,128)(2,1)} %bitcast.12, bf16[]{:T(256)} %constant.2.clone.1), padding=0_8x0_0 | pad | bytes 49154 | tf_op jit(solution)/shard_map/jit(_pad)/pad | solution.py:600
  5.2 113.8 %shard_map.120 = (f32[48,1024]{1,0:T(8,128)}, f32[1,1024]{1,0:T(1,128)}, f32[1024,8]{1,0:T(8,128)}, f32[8,1]{1,0:T(8,128)}) custom-call(bf16[128,4096]{1,0:T(8,128)(2,1)} %bitcast.9, bf16[128,1024]{1,0:T(8,128)(2,1)} %bitcast.10, bf16[128,1024]{1,0:T(8,128)(2,1)} %bitcast.11, bf16[6144,1024]{1,0:T(8,128)(2,1)} %w_ref.1, f32[1,1024]{1,0:T(1,128)} %bitcast.14, ...), custom_call_target="tpu_custom_call" | custom-call | tf_op jit(solution)/shard_map/pallas_call | solution.py:615
  119.0 1.3 %reduce = f32[8]{0:T(128)} reduce(f32[8,1]{1,0:T(8,128)} %get-tuple-element.11, f32[]{:T(128)} %constant.11), dimensions={1}, to_apply=%get-tuple-element.11.reduce_sub_computation | reduce | bytes 68 | tf_op jit(solution)/shard_map/pallas_call | solution.py:615
  120.3 1.8 %copy.18 = f32[1024,8]{0,1:T(8,128)} copy(f32[1024,8]{1,0:T(8,128)} %get-tuple-element.22) | data formatting | bytes 65536
  122.1 1.6 %copy.22 = f32[48,1024]{1,0:T(8,128)} copy(f32[48,1024]{1,0:T(8,128)} %get-tuple-element.28) | data formatting | bytes 393216
  123.8 1.3 %copy.23 = f32[1024]{0:T(1024)} copy(f32[1024]{0:T(1024)} %bitcast.13) | data formatting | bytes 8192

commit v2 on v1

--- a/solution.py
+++ b/solution.py
@@ -13,6 +13,7 @@
 MESH = pl.DeviceIdType.MESH
 SIDE = 4
 ROUNDS = 2
+FIXED = 54000.0
 GRAN = 16
 LOG2E = 1.4426950408889634
 
@@ -41,12 +42,9 @@
     wt_ref,
     bias_ref,
     order_ref,
-    inv_ref,
     limit_ref,
     grad_ref,
-    gb_ref,
-    gw_ref,
-    ob_ref,
+    small_ref,
     win,
     qg,
     kg,
@@ -61,6 +59,9 @@
     colacc,
     mp,
     mr,
+    predg,
+    rs,
+    dq,
     dg,
     otc,
     otr,
@@ -73,6 +74,7 @@
     xr,
     fin,
     fout,
+    inv,
     wsem,
     qsem,
     ksem,
@@ -80,6 +82,7 @@
     qpsem,
     vsem,
     msem,
+    dsem,
     asem,
     osem,
     bsem,
@@ -92,7 +95,7 @@
     mb = lax.axis_index("batch")
     rows, kd = k_ref.shape
     hidden = slope.shape[1]
-    heads = wt_ref.shape[0] // 2
+    heads = wt_ref.shape[0]
     head = kd // heads
     chips = n // 2
     chip = me // 2
@@ -172,6 +175,14 @@
     kg[me] = k_ref[:, at(chip // 2, head)]
     ft[pl.ds(value_base, vpart), at(chip, rows)] = vt[at(chip, vpart), :]
 
+    def invert(p, carry):
+        found = jnp.int32(0)
+        for s in range(n):
+            found = jnp.where(order_ref[0, s] == p, jnp.int32(s), found)
+        inv[p] = found
+        return carry
+
+    lax.fori_loop(0, n, invert, 0)
     load.wait()
     tile = hidden // 4
 
@@ -191,11 +202,105 @@
         return carry
 
     lax.fori_loop(0, 4, project, 0)
-    wt = wt_ref[...]
-    pred = (
+    blocks = hidden // rows
+    for j in range(blocks):
+        fixed = jnp.floor((slope[:, j * rows : (j + 1) * rows] - 0.5) * FIXED + 0.5)
+        dq[j, at(chip, rows), :] = fixed.astype(jnp.int32).astype(jnp.int16)
+
+    classes = blocks // ROUNDS
+    gathered = {}
+
+    def place(k, a, b):
+        dy, dz = (a, b) if k < 2 else (b, a)
+        return lax.rem(cy + SIDE - dy, SIDE) * SIDE + lax.rem(cz + SIDE - dz, SIDE)
+
+    def forward(r, k, a, b, axis, move):
+        along_y = (axis == 0) == (k < 2)
+        if along_y:
+            to = lax.rem(cy + SIDE + move, SIDE) * SIDE + cz
+        else:
+            to = cy * SIDE + lax.rem(cz + SIDE + move, SIDE)
+        a2, b2 = ((a + move) % SIDE, b) if axis == 0 else (a, (b + move) % SIDE)
+        part = dq.at[r * classes + k, at(place(k, a, b), rows)]
+        copy = copy_to(part, part, asem, (r, k, a2 * SIDE + b2), {"seq": to * 2 + core})
+        copy.start()
+        gathered[r, k, a2, b2] = copy
+
+    def arrive(r, k, a, b):
+        gathered[r, k, a, b].wait_recv()
+
+    def toward(k):
+        return (1, 1, 3) if k % 2 == 0 else (-1, 3, 1)
+
+    def stage0(r):
+        for k in range(classes):
+            for axis in (0, 1):
+                for move in (1, -1):
+                    forward(r, k, 0, 0, axis, move)
+
+    def stage1(r):
+        for k in range(classes):
+            move, near, far = toward(k)
+            arrive(r, k, near, 0)
+            forward(r, k, near, 0, 0, move)
+            forward(r, k, near, 0, 1, 1)
+            forward(r, k, near, 0, 1, -1)
+        for k in range(classes):
+            move, near, far = toward(k)
+            arrive(r, k, far, 0)
+            forward(r, k, far, 0, 1, 1)
+            forward(r, k, far, 0, 1, -1)
+
+    def stage2(r):
+        for k in range(classes):
+            move, near, far = toward(k)
+            arrive(r, k, 0, near)
+            forward(r, k, 0, near, 1, move)
+        for k in range(classes):
+            arrive(r, k, 2, 0)
+            forward(r, k, 2, 0, 1, 1)
+            forward(r, k, 2, 0, 1, -1)
+
+    def stage3(r):
+        for a in (0, 1):
+            for k in range(classes):
+                move, near, far = toward(k)
+                line = near if a == 0 else far
+                arrive(r, k, line, near)
+                forward(r, k, line, near, 1, move)
+
+    def stage4(r):
+        for k in range(classes):
+            move, near, far = toward(k)
+            arrive(r, k, 2, near)
+            forward(r, k, 2, near, 1, move)
+
+    def stage5(r):
+        for k in range(classes):
+            move, near, far = toward(k)
+            for a in range(SIDE):
+                arrive(r, k, a, far)
+                arrive(r, k, a, 2)
+
+    stage0(0)
+    stage0(1)
+    wt32 = wt_ref[...].astype(F32)
+    wt = jnp.concatenate([wt32, jnp.zeros_like(wt32)], axis=0).astype(BF16)
+    group_index = lax.broadcasted_iota(jnp.int32, (heads, 1), 0)
+    bias = jnp.zeros((heads, 1), F32)
+    for g in range(heads):
+        bias = jnp.where(group_index == g, bias_ref[0, g], bias)
+    predg[chip] = (
         lax.dot_general(wt, act[...], (((1,), (1,)), ((), ())), preferred_element_type=F32)[:heads]
-        + bias_ref[...]
+        + bias
     )
+    preds_sent = []
+    for d in range(1, chips):
+        copy = copy_to(
+            predg.at[chip], predg.at[chip], dsem, (d,), {"seq": chip_peer(d) * 2 + core}
+        )
+        copy.start()
+        preds_sent.append(copy)
 
     for d in range(1, chips):
         key_far[d - 1].wait_recv()
@@ -223,7 +328,7 @@
     limit = limit_ref[0]
 
     def sort_keys(p, carry):
-        ks[at(p, rows), :] = kg[inv_ref[0, p]]
+        ks[at(p, rows), :] = kg[inv[p]]
         return carry
 
     lax.fori_loop(0, n, sort_keys, 0)
@@ -237,7 +342,7 @@
 
         def query_block(t, carry, w=w):
             block = w * step + t
-            queries = qg[inv_ref[0, block]]
+            queries = qg[inv[block]]
             best = None
             for kc in range(w + 1):
                 score = lax.dot_general(
@@ -269,16 +374,31 @@
             return carry
 
         lax.fori_loop(0, step, query_block, 0)
+        if w == 2:
+            stage1(0)
+        elif w == 3:
+            stage1(1)
+        elif w == 4:
+            stage2(0)
+            stage3(0)
+        elif w == 5:
+            stage2(1)
+            stage3(1)
+        elif w == 6:
+            stage4(0)
+            stage4(1)
 
     for t in range(n):
-        mp[t] = colacc[order_ref[0, t]]
+        mp[t % 2, t // 2 : t // 2 + 1, :] = jnp.sum(
+            colacc[order_ref[0, t]], axis=0, keepdims=True
+        )
     mass_sent = []
     for d in range(1, n):
         to = seq_peer(d)
-        copy = copy_to(mp.at[to], mr.at[me], msem, (d,), {"seq": to})
+        copy = copy_to(mp.at[to % 2], mr.at[me], msem, (d,), {"seq": to})
         copy.start()
         mass_sent.append(copy)
-    mr[me] = mp[me]
+    mr[me] = mp[core]
 
     for copy in queries_passed:
         copy.wait_recv()
@@ -294,137 +414,42 @@
     lax.fori_loop(0, chips, turn_features, 0)
     ft[pl.ds(2 * head, vpart), :] = kt[at(chip % 2, vpart), :]
 
+    for copy in preds_sent:
+        copy.wait_recv()
+    for r in range(ROUNDS):
+        stage5(r)
     for copy in mass_sent:
         copy.wait_recv()
     per_group = n // heads
-    sums = []
+    labels = []
     for g in range(heads):
         value = mr[g * per_group]
         for j in range(1, per_group):
             value = value + mr[g * per_group + j]
-        sums.append(jnp.sum(value, axis=0, keepdims=True))
-    mass = jnp.concatenate(sums, axis=0)
+        labels.append(jnp.log1p(value))
     lane = lax.broadcasted_iota(jnp.int32, (1, rows), 1)
-    live_row = (lane + order_ref[0, me] * rows < limit).astype(F32)
-    resid = ((pred - jnp.log1p(mass)) * live_row * norm).astype(BF16)
-    resid32 = resid.astype(F32)
-    resid_all = jnp.concatenate([resid32, jnp.zeros_like(resid32)], axis=0)
-    back = jnp.dot(resid_all.T.astype(BF16), wt, preferred_element_type=F32)
-    delta = (back * slope[...]).astype(BF16)
-    blocks = hidden // rows
-    for j in range(blocks):
-        dg[j, at(chip, rows), :] = delta[:, j * rows : (j + 1) * rows]
-
-    classes = blocks // ROUNDS
-    gathered = {}
-
-    def place(k, a, b):
-        dy, dz = (a, b) if k < 2 else (b, a)
-        return lax.rem(cy + SIDE - dy, SIDE) * SIDE + lax.rem(cz + SIDE - dz, SIDE)
-
-    def forward(r, k, a, b, axis, move):
-        along_y = (axis == 0) == (k < 2)
-        if along_y:
-            to = lax.rem(cy + SIDE + move, SIDE) * SIDE + cz
-        else:
-            to = cy * SIDE + lax.rem(cz + SIDE + move, SIDE)
-        a2, b2 = ((a + move) % SIDE, b) if axis == 0 else (a, (b + move) % SIDE)
-        part = dg.at[r * classes + k, at(place(k, a, b), rows)]
-        copy = copy_to(part, part, asem, (r, k, a2 * SIDE + b2), {"seq": to * 2 + core})
-        copy.start()
-        gathered[r, k, a2, b2] = copy
-
-    def arrive(r, k, a, b):
-        gathered[r, k, a, b].wait_recv()
-
-    def toward(k):
-        return (1, 1, 3) if k % 2 == 0 else (-1, 3, 1)
-
-    def stage0(r):
-        for k in range(classes):
-            for axis in (0, 1):
-                for move in (1, -1):
-                    forward(r, k, 0, 0, axis, move)
-
-    def stage1(r):
-        for k in range(classes):
-            move, near, far = toward(k)
-            arrive(r, k, near, 0)
-            forward(r, k, near, 0, 0, move)
-            forward(r, k, near, 0, 1, 1)
-            forward(r, k, near, 0, 1, -1)
-        for k in range(classes):
-            move, near, far = toward(k)
-            arrive(r, k, far, 0)
-            forward(r, k, far, 0, 1, 1)
-            forward(r, k, far, 0, 1, -1)
-
-    def stage2(r):
-        for k in range(classes):
-            move, near, far = toward(k)
-            arrive(r, k, 0, near)
-            forward(r, k, 0, near, 1, move)
-        for k in range(classes):
-            arrive(r, k, 2, 0)
-            forward(r, k, 2, 0, 1, 1)
-            forward(r, k, 2, 0, 1, -1)
-
-    def stage3(r):
-        for a in (0, 1):
-            for k in range(classes):
-                move, near, far = toward(k)
-                line = near if a == 0 else far
-                arrive(r, k, line, near)
-                forward(r, k, line, near, 1, move)
-
-    def stage4(r):
-        for k in range(classes):
-            move, near, far = toward(k)
-            arrive(r, k, 2, near)
-            forward(r, k, 2, near, 1, move)
-
-    def stage5(r):
-        for k in range(classes):
-            move, near, far = toward(k)
-            for a in range(SIDE):
-                arrive(r, k, a, far)
-                arrive(r, k, a, 2)
-
-    stage0(0)
-    out_term = jnp.dot(resid_all.astype(BF16), act[...], preferred_element_type=F32)
-    width = hidden // n
-    bias_sum = jnp.broadcast_to(jnp.sum(resid32, axis=1, keepdims=True), (heads, width))
-    delta_sum = jnp.sum(delta.astype(F32), axis=0, keepdims=True)
-    for p in range(n):
-        otc[p, :heads] = out_term[:heads, p * width : (p + 1) * width]
-        otc[p, heads : 2 * heads] = bias_sum
-        otc[p, 2 * heads :] = jnp.broadcast_to(
-            delta_sum[:, p * width : (p + 1) * width], (heads, width)
-        )
-    stage1(0)
-    stage0(1)
-    first = []
-    for d in range(1, n):
-        to = seq_peer(d)
-        copy = copy_to(otc.at[to], otr.at[d], osem, (d,), {"seq": to})
-        copy.start()
-        first.append(copy)
-    stage2(0)
-    stage3(0)
-    stage1(1)
-    small = otc[me]
-    for d in range(1, n):
-        first[d - 1].wait_recv()
-        small = small + otr[d]
-    obs[...] = small
-    second = []
-    for d in range(1, nb):
-        copy = copy_to(obs, obr.at[d], bsem, (d,), {"batch": batch_peer(d)})
-        copy.start()
-        second.append(copy)
-    stage4(0)
-    stage2(1)
-    stage5(0)
+    for s in range(chips):
+        label = jnp.concatenate([part[s : s + 1] for part in labels], axis=0)
+        live_row = (lane + order_ref[0, 2 * s + core] * rows < limit).astype(F32)
+        resid = ((predg[s] - label) * live_row * norm).astype(BF16).astype(F32)
+        rs[s] = jnp.concatenate([resid, jnp.zeros_like(resid)], axis=0)
+
+    def delta_round(r):
+        base = r * classes
+
+        def tokens(s, carry):
+            back = jnp.dot(
+                rs[s].T.astype(BF16),
+                wt[:, base * rows : (base + classes) * rows],
+                preferred_element_type=F32,
+            )
+            for j in range(classes):
+                held = dq[base + j, at(s, rows), :].astype(jnp.int32).astype(F32)
+                value = back[:, j * rows : (j + 1) * rows] * (held * (1.0 / FIXED) + 0.5)
+                dg[base + j, at(s, rows), :] = value.astype(BF16)
+            return carry
+
+        lax.fori_loop(0, chips, tokens, 0)
 
     half = ft.shape[0] // 2
     piece = hidden // ROUNDS
@@ -529,10 +554,43 @@
             def _(r=r, e=e):
                 fout[r, e] = fin[r, e]
 
+    delta_round(0)
     swap(0)
-    stage3(1)
+    resid32 = rs[chip]
+    out_term = jnp.dot(resid32.astype(BF16), act[...], preferred_element_type=F32)
+    width = hidden // n
+    bias_sum = jnp.broadcast_to(jnp.sum(resid32[:heads], axis=1, keepdims=True), (heads, width))
+    delta = (
+        jnp.dot(resid32.T.astype(BF16), wt, preferred_element_type=F32) * slope[...]
+    ).astype(BF16)
+    delta_sum = jnp.sum(delta.astype(F32), axis=0, keepdims=True)
+    for p in range(n):
+        otc[p, :heads] = out_term[:heads, p * width : (p + 1) * width]
+        otc[p, heads : 2 * heads] = bias_sum
+        otc[p, 2 * heads :] = jnp.broadcast_to(
+            delta_sum[:, p * width : (p + 1) * width], (heads, width)
+        )
+    first = []
+    for d in range(1, n):
+        to = seq_peer(d)
+        copy = copy_to(otc.at[to], otr.at[d], osem, (d,), {"seq": to})
+        copy.start()
+        first.append(copy)
     reduce_chip(0)
-    stage4(1)
+    delta_round(1)
+    swap(1)
+    small = otc[me]
+    for d in range(1, n):
+        first[d - 1].wait_recv()
+        small = small + otr[d]
+    obs[...] = small
+    second = []
+    for d in range(1, nb):
+        copy = copy_to(obs, obr.at[d], bsem, (d,), {"batch": batch_peer(d)})
+        copy.start()
+        second.append(copy)
+    reduce_chip(1)
+    finish(0)
     small = obs[...]
     for d in range(1, nb):
         second[d - 1].wait_recv()
@@ -543,16 +601,17 @@
         copy = copy_to(ofin.at[me], ofin.at[me], hsem, (d,), {"seq": seq_peer(d)})
         copy.start()
         third.append(copy)
-    stage5(1)
-    swap(1)
-    finish(0)
-    reduce_chip(1)
+    finish(1)
     for copy in third:
         copy.wait_recv()
-    gw_ref[...] = jnp.concatenate([ofin[p, :heads] for p in range(n)], axis=1).T
-    ob_ref[...] = ofin[0, heads : 2 * heads, :1]
-    gb_ref[...] = jnp.concatenate([ofin[p, 2 * heads : 2 * heads + 1] for p in range(n)], axis=1)
-    finish(1)
+    small_ref[:heads] = jnp.concatenate([ofin[p, :heads] for p in range(n)], axis=1)
+    gb = jnp.concatenate([ofin[p, 2 * heads : 2 * heads + 1] for p in range(n)], axis=1)
+    column = ofin[0, heads : 2 * heads, :1]
+    lane_all = lax.broadcasted_iota(jnp.int32, (heads, hidden), 1)
+    ob = jnp.sum(jnp.where(lane_all == group_index, column, 0.0), axis=0, keepdims=True)
+    small_ref[heads:] = jnp.concatenate(
+        [gb, ob, jnp.zeros((heads - 2, hidden), F32)], axis=0
+    )
     for r in range(ROUNDS):
         for e in range(share_rows):
 
@@ -568,6 +627,7 @@
         + queries_passed
         + values_sent
         + mass_sent
+        + preds_sent
         + list(gathered.values())
         + first
         + second
@@ -582,6 +642,14 @@
             @pl.when(owner_of(e) != me)
             def _(r=r, e=e):
                 final_copy(r, e).wait_send()
+
+
+def emit(grad_in, small_in, grad_ref, gw_ref, gb_ref, ob_ref):
+    heads = gw_ref.shape[0]
+    grad_ref[...] = grad_in[...]
+    gw_ref[...] = small_in[:heads]
+    gb_ref[...] = small_in[heads : heads + 1]
+    ob_ref[...] = small_in[heads + 1 : heads + 2, :heads]
 
 
 def on_device(queries, keys, values, lengths, block_pos, w_in, b_in, output_weight, output_bias):
@@ -597,7 +665,6 @@
     head = kd // heads
     scale = 1.0 / math.sqrt(head)
     norm = 1.0 / math.sqrt(nb * n * rows)
-    wt = jnp.pad(output_weight.T, ((0, heads), (0, 0)))
     vmem = pl.BlockSpec(memory_space=pltpu.VMEM)
     total = n * rows
     chips = n // 2
@@ -607,24 +674,18 @@
     piece = hidden // ROUNDS
     grans = chip_feat // 2 // GRAN
     share_rows = grans // nb
-    places = jnp.arange(n, dtype=jnp.int32)
-    inverse = jnp.sum(
-        jnp.where(block_pos[0][None, :] == places[:, None], places[None, :], 0), axis=1
-    )[None, :]
     dma = pltpu.SemaphoreType.DMA
-    grad, gb, gw, ob = pl.pallas_call(
+    grad, small = pl.pallas_call(
         functools.partial(kernel, n, nb, norm, scale),
         out_shape=(
             jax.ShapeDtypeStruct((part, hidden), F32),
-            jax.ShapeDtypeStruct((1, hidden), F32),
-            jax.ShapeDtypeStruct((hidden, heads), F32),
-            jax.ShapeDtypeStruct((heads, 1), F32),
+            jax.ShapeDtypeStruct((2 * heads, hidden), F32),
         ),
         in_specs=[vmem] * 3
         + [pl.BlockSpec(memory_space=pl.ANY)]
-        + [vmem] * 3
+        + [vmem] * 2
         + [pl.BlockSpec(memory_space=pltpu.SMEM)] * 3,
-        out_specs=(vmem, vmem, vmem, vmem),
+        out_specs=(vmem, vmem),
         scratch_shapes=[
             pltpu.VMEM((feat, hidden), BF16),
             pltpu.VMEM((n, rows, head), BF16),
@@ -638,8 +699,11 @@
             pltpu.VMEM((rows, hidden), BF16),
             pltpu.VMEM((rows, total), F32),
             pltpu.VMEM((n, 8, rows), F32),
-            pltpu.VMEM((n, 8, rows), F32),
-            pltpu.VMEM((n, 8, rows), F32),
+            pltpu.VMEM((2, chips, rows), F32),
+            pltpu.VMEM((n, chips, rows), F32),
+            pltpu.VMEM((chips, heads, rows), F32),
+            pltpu.VMEM((chips, 2 * heads, rows), F32),
+            pltpu.VMEM((hidden // rows, total // 2, rows), jnp.int16),
             pltpu.VMEM((hidden // rows, total // 2, rows), BF16),
             pltpu.VMEM((n, 3 * heads, width), F32),
             pltpu.VMEM((n, 3 * heads, width), F32),
@@ -652,6 +716,7 @@
             pltpu.VMEM((ROUNDS, nb, share_rows, GRAN, piece), F32),
             pltpu.VMEM((ROUNDS, share_rows, GRAN, piece), F32),
             pltpu.VMEM((ROUNDS, share_rows, GRAN, piece), F32),
+            pltpu.SMEM((n,), jnp.int32),
             dma,
             dma((2, n)),
             dma((2, chips)),
@@ -659,6 +724,7 @@
             dma((2, chips)),
             dma((2, chips)),
             dma((2, n)),
+            dma((2, chips)),
             dma((2, ROUNDS, hidden // rows // ROUNDS, SIDE * SIDE)),
             dma((2, n)),
             dma((2, nb)),
@@ -676,13 +742,23 @@
         v_rows,
         w_in,
         b_in[None, :],
-        wt,
-        output_bias[:, None],
+        output_weight.T,
+        output_bias[None, :],
         block_pos,
-        inverse,
         lengths,
     )
-    return (grad, gb[0], gw, ob[:, 0])
+    grad, gw, gb, ob = pl.pallas_call(
+        emit,
+        out_shape=(
+            jax.ShapeDtypeStruct((part, hidden), F32),
+            jax.ShapeDtypeStruct((heads, hidden), F32),
+            jax.ShapeDtypeStruct((1, hidden), F32),
+            jax.ShapeDtypeStruct((1, heads), F32),
+        ),
+        in_specs=[vmem] * 2,
+        out_specs=(vmem,) * 4,
+    )(grad, small)
+    return (grad, gb[0], gw.T, ob[0])
 
 
 def solution(mesh):

time: 126 us -> 99 us (0.79)
  Pallas kernels: 114 us -> 96.7 us
  local copies, waits for them, and re-layouts: 7.37 us -> 0 us
  other arithmetic: 2.6 us -> 0 us
    pallas_call x1, Pallas kernels: 114 us -> 95 us  [on_device(): pl.pallas_call(functools.partial(kernel, n, nb, norm, scale), out_shape=(...]
    unnamed x3 -> x0, local copies, waits for them, and re-layouts: 4.71 us -> none
    pallas_call x0 -> x1, Pallas kernels: none -> 1.63 us  [on_device(): pl.pallas_call(emit, out_shape=(jax.ShapeDtypeStruct((part, hidden), F32)...]
    pad x1 -> x0, local copies, waits for them, and re-layouts: 1.33 us -> none  [on_device(): wt = jnp.pad(output_weight.T, ((0, heads), (0, 0)))]
    broadcast_in_dim x1 -> x0, local copies, waits for them, and re-layouts: 1.32 us -> none  [on_device(): output_bias[:, None]]
    pallas_call x1 -> x0, other arithmetic: 1.31 us -> none  [on_device(): pl.pallas_call(functools.partial(kernel, n, nb, norm, scale), out_shape=(...]
    reduce_sum x1 -> x0, other arithmetic: 1.28 us -> none  [on_device(): jnp.sum(jnp.where(block_pos[0][None, :] == places[:, None], places[None,...]
where the time goes in v2:
time: 99 us; the launch traced here: 98 us
  Pallas kernels  96.7 us (98%)
  between operations  1.29 us (1%)
    pallas_call x1, Pallas kernels, on_device(): pl.pallas_call(functools.partial(kernel, n, nb, norm, scale), out_shape=(...  95 us

profile of v2, /device:TPU:8, one launch (start us, length us, event | category | flops | bytes accessed | tf_op | source)
XLA Modules:
  0.0 98.0 jit_solution(11986435632440198436)
XLA Ops:
  1.3 95.0 %shard_map.120 = (f32[48,1024]{1,0:T(8,128)}, f32[16,1024]{1,0:T(8,128)}) custom-call(bf16[128,4096]{1,0:T(8,128)(2,1)} %bitcast.9, bf16[128,1024]{1,0:T(8,128)(2,1)} %bitcast.10, bf16[128,1024]{1,0:T(8,128)(2,1)} %bitcast.11, bf16[6144,1024]{1,0:T(8,128)(2,1)} %w_ref.1, f32[1,1024]{1,0:T(1,128)} %bitcast.13, bf16[8,1024]{1,0:T(8,128)(2,1)} %bitcast.12, ...), custom_call_target="tpu_custom_call" | custom-call | tf_op jit(solution)/shard_map/pallas_call | solution.py:678
  96.3 1.6 %shard_map.121 = (f32[48,1024]{1,0:T(8,128)}, f32[8,1024]{1,0:T(8,128)}, f32[1,1024]{1,0:T(1,128)}, f32[1,8]{1,0:T(1,128)}) custom-call(f32[48,1024]{1,0:T(8,128)} %get-tuple-element.10.grad_in, f32[16,1024]{1,0:T(8,128)} %get-tuple-element.11.small_in), custom_call_target="tpu_custom_call" | custom-call | tf_op jit(solution)/shard_map/pallas_call | solution.py:750

commit v3 on v2

--- a/solution.py
+++ b/solution.py
@@ -13,9 +13,21 @@
 MESH = pl.DeviceIdType.MESH
 SIDE = 4
 ROUNDS = 2
+CLASSES = 4
 FIXED = 54000.0
 GRAN = 16
 LOG2E = 1.4426950408889634
+
+
+def waiter(ref, sems, index):
+    return pltpu.make_async_remote_copy(
+        src_ref=ref,
+        dst_ref=ref,
+        send_sem=sems.at[(0, *index)],
+        recv_sem=sems.at[(1, *index)],
+        device_id={"seq": lax.axis_index("seq")},
+        device_id_type=MESH,
+    )
 
 
 def copy_to(src, dst, sems, index, target):
@@ -136,40 +148,31 @@
     lax.fori_loop(0, kd // head, turn_values, 0)
     pl.semaphore_wait(barrier, n + nb - 2)
 
-    key_far = []
     for d in range(1, chips):
         to = chip_peer(d)
         copy = copy_to(
-            k_ref.at[:, at(to // 2, head)], kg.at[me], ksem, (d,), {"seq": to * 2 + core}
+            k_ref.at[:, at(to // 2, head)], kg.at[me], ksem, (), {"seq": to * 2 + core}
         )
         copy.start()
-        key_far.append(copy)
-    key_near = [
-        copy_to(k_ref.at[:, at(chip // 2, head)], kg.at[me], kpsem, (0,), {"seq": pair})
-    ]
-    key_near[0].start()
-    queries_sent = []
+    copy_to(k_ref.at[:, at(chip // 2, head)], kg.at[me], kpsem, (), {"seq": pair}).start()
     for d in range(1, n):
         to = seq_peer(d)
         copy = copy_to(
-            q_ref.at[:, at(to, head)], qg.at[me], qsem, (d,), {"seq": to}
+            q_ref.at[:, at(to, head)], qg.at[me], qsem, (), {"seq": to}
         )
         copy.start()
-        queries_sent.append(copy)
     vpart = kd // chips
     value_base = 2 * head + vpart
-    values_sent = []
     for d in range(1, chips):
         to = chip_peer(d)
         copy = copy_to(
             vt.at[at(to, vpart)],
             ft.at[pl.ds(value_base, vpart), at(chip, rows)],
             vsem,
-            (d,),
+            (),
             {"seq": to * 2 + core},
         )
         copy.start()
-        values_sent.append(copy)
     qg[me] = q_ref[:, at(me, head)]
     qo[at(chip, rows), :] = q_ref[:, at(pair, head)]
     kg[me] = k_ref[:, at(chip // 2, head)]
@@ -202,88 +205,104 @@
         return carry
 
     lax.fori_loop(0, 4, project, 0)
-    blocks = hidden // rows
-    for j in range(blocks):
-        fixed = jnp.floor((slope[:, j * rows : (j + 1) * rows] - 0.5) * FIXED + 0.5)
-        dq[j, at(chip, rows), :] = fixed.astype(jnp.int32).astype(jnp.int16)
-
-    classes = blocks // ROUNDS
-    gathered = {}
+    lanes = hidden // CLASSES
+    for k in range(CLASSES):
+        fixed = jnp.floor((slope[:, k * lanes : (k + 1) * lanes] - 0.5) * FIXED + 0.5)
+        dq[k, at(chip, rows), :] = fixed.astype(jnp.int32).astype(jnp.int16)
+
+    LAST = SIDE + 3
 
     def place(k, a, b):
         dy, dz = (a, b) if k < 2 else (b, a)
         return lax.rem(cy + SIDE - dy, SIDE) * SIDE + lax.rem(cz + SIDE - dz, SIDE)
 
-    def forward(r, k, a, b, axis, move):
+    def toward(k):
+        return (1, 1, 3) if k % 2 == 0 else (-1, 3, 1)
+
+    def slot(k, a, b):
+        move, near, far = toward(k)
+        if b == 0:
+            return a - 1
+        return 3 + a if b == near else LAST
+
+    def forward(k, a, b, axis, move):
         along_y = (axis == 0) == (k < 2)
         if along_y:
             to = lax.rem(cy + SIDE + move, SIDE) * SIDE + cz
         else:
             to = cy * SIDE + lax.rem(cz + SIDE + move, SIDE)
         a2, b2 = ((a + move) % SIDE, b) if axis == 0 else (a, (b + move) % SIDE)
-        part = dq.at[r * classes + k, at(place(k, a, b), rows)]
-        copy = copy_to(part, part, asem, (r, k, a2 * SIDE + b2), {"seq": to * 2 + core})
-        copy.start()
-        gathered[r, k, a2, b2] = copy
-
-    def arrive(r, k, a, b):
-        gathered[r, k, a, b].wait_recv()
-
-    def toward(k):
-        return (1, 1, 3) if k % 2 == 0 else (-1, 3, 1)
-
-    def stage0(r):
-        for k in range(classes):
-            for axis in (0, 1):
+        part = dq.at[k, at(place(k, a, b), rows)]
+        pltpu.make_async_remote_copy(
+            src_ref=part,
+            dst_ref=part,
+            send_sem=asem.at[CLASSES, 0],
+            recv_sem=asem.at[k, slot(k, a2, b2)],
+            device_id={"seq": to * 2 + core},
+            device_id_type=MESH,
+        ).start()
+
+    def gathered(ref, k, i):
+        return pltpu.make_async_remote_copy(
+            src_ref=ref,
+            dst_ref=ref,
+            send_sem=asem.at[CLASSES, 0],
+            recv_sem=asem.at[k, i],
+            device_id={"seq": me},
+            device_id_type=MESH,
+        )
+
+    def arrive(k, a, b):
+        gathered(dq.at[k, at(place(k, a, b), rows)], k, slot(k, a, b)).wait_recv()
+
+    def stage0():
+        for axis in (0, 1):
+            for k in range(CLASSES):
                 for move in (1, -1):
-                    forward(r, k, 0, 0, axis, move)
-
-    def stage1(r):
-        for k in range(classes):
+                    forward(k, 0, 0, axis, move)
+
+    def stage1():
+        for k in range(CLASSES):
             move, near, far = toward(k)
-            arrive(r, k, near, 0)
-            forward(r, k, near, 0, 0, move)
-            forward(r, k, near, 0, 1, 1)
-            forward(r, k, near, 0, 1, -1)
-        for k in range(classes):
+            arrive(k, near, 0)
+            forward(k, near, 0, 0, move)
+            forward(k, near, 0, 1, 1)
+            forward(k, near, 0, 1, -1)
+        for k in range(CLASSES):
             move, near, far = toward(k)
-            arrive(r, k, far, 0)
-            forward(r, k, far, 0, 1, 1)
-            forward(r, k, far, 0, 1, -1)
-
-    def stage2(r):
-        for k in range(classes):
+            arrive(k, far, 0)
+            forward(k, far, 0, 1, 1)
+            forward(k, far, 0, 1, -1)
+
+    def stage2():
+        for k in range(CLASSES):
             move, near, far = toward(k)
-            arrive(r, k, 0, near)
-            forward(r, k, 0, near, 1, move)
-        for k in range(classes):
-            arrive(r, k, 2, 0)
-            forward(r, k, 2, 0, 1, 1)
-            forward(r, k, 2, 0, 1, -1)
-
-    def stage3(r):
+            arrive(k, 0, near)
+            forward(k, 0, near, 1, move)
+        for k in range(CLASSES):
+            arrive(k, 2, 0)
+            forward(k, 2, 0, 1, 1)
+            forward(k, 2, 0, 1, -1)
+
+    def stage3():
         for a in (0, 1):
-            for k in range(classes):
+            for k in range(CLASSES):
                 move, near, far = toward(k)
                 line = near if a == 0 else far
-                arrive(r, k, line, near)
-                forward(r, k, line, near, 1, move)
-
-    def stage4(r):
-        for k in range(classes):
+                arrive(k, line, near)
+                forward(k, line, near, 1, move)
+
+    def stage4():
+        for k in range(CLASSES):
             move, near, far = toward(k)
-            arrive(r, k, 2, near)
-            forward(r, k, 2, near, 1, move)
-
-    def stage5(r):
-        for k in range(classes):
-            move, near, far = toward(k)
-            for a in range(SIDE):
-                arrive(r, k, a, far)
-                arrive(r, k, a, 2)
-
-    stage0(0)
-    stage0(1)
+            arrive(k, 2, near)
+            forward(k, 2, near, 1, move)
+
+    def stage5():
+        for k in range(CLASSES):
+            gathered(dq.at[k, pl.ds(0, 2 * SIDE * rows)], k, LAST).wait_recv()
+
+    stage0()
     wt32 = wt_ref[...].astype(F32)
     wt = jnp.concatenate([wt32, jnp.zeros_like(wt32)], axis=0).astype(BF16)
     group_index = lax.broadcasted_iota(jnp.int32, (heads, 1), 0)
@@ -294,36 +313,38 @@
         lax.dot_general(wt, act[...], (((1,), (1,)), ((), ())), preferred_element_type=F32)[:heads]
         + bias
     )
-    preds_sent = []
     for d in range(1, chips):
         copy = copy_to(
-            predg.at[chip], predg.at[chip], dsem, (d,), {"seq": chip_peer(d) * 2 + core}
+            predg.at[chip], predg.at[chip], dsem, (), {"seq": chip_peer(d) * 2 + core}
         )
         copy.start()
-        preds_sent.append(copy)
-
+
+    waits = {
+        "key_far": waiter(kg.at[pl.ds(0, chips - 1)], ksem, ()),
+        "key_near": waiter(kg.at[pl.ds(0, chips)], kpsem, ()),
+        "query": waiter(qg.at[pl.ds(0, n - 1)], qsem, ()),
+        "query_near": waiter(qo.at[pl.ds(0, (chips - 1) * rows)], qpsem, ()),
+        "value": waiter(
+            ft.at[pl.ds(value_base, vpart), pl.ds(0, (chips - 1) * rows)], vsem, ()
+        ),
+        "mass": waiter(mr.at[pl.ds(0, n - 1)], msem, ()),
+        "pred": waiter(predg.at[pl.ds(0, chips - 1)], dsem, ()),
+    }
+    waits["key_far"].wait_recv()
     for d in range(1, chips):
-        key_far[d - 1].wait_recv()
         held = kg.at[chip_source(d) * 2 + core]
-        copy = copy_to(held, held, kpsem, (d,), {"seq": pair})
-        copy.start()
-        key_near.append(copy)
-    for d in range(1, n):
-        queries_sent[d - 1].wait_recv()
-    queries_passed = []
+        copy_to(held, held, kpsem, (), {"seq": pair}).start()
+    waits["query"].wait_recv()
     for d in range(1, chips):
         source = chip_source(d)
-        copy = copy_to(
+        copy_to(
             qg.at[source * 2 + (1 - core)],
             qo.at[at(source, rows)],
             qpsem,
-            (d,),
+            (),
             {"seq": pair},
-        )
-        copy.start()
-        queries_passed.append(copy)
-    for copy in key_near:
-        copy.wait_recv()
+        ).start()
+    waits["key_near"].wait_recv()
 
     limit = limit_ref[0]
 
@@ -373,37 +394,30 @@
                 colacc[kb] += jnp.sum(part.reshape(rows // 8, 8, rows), axis=0)
             return carry
 
-        lax.fori_loop(0, step, query_block, 0)
+        if w == n // step - 1:
+            lax.fori_loop(0, step // 2, query_block, 0)
+            stage4()
+            lax.fori_loop(step // 2, step, query_block, 0)
+        else:
+            lax.fori_loop(0, step, query_block, 0)
         if w == 2:
-            stage1(0)
-        elif w == 3:
-            stage1(1)
+            stage1()
         elif w == 4:
-            stage2(0)
-            stage3(0)
-        elif w == 5:
-            stage2(1)
-            stage3(1)
+            stage2()
         elif w == 6:
-            stage4(0)
-            stage4(1)
+            stage3()
 
     for t in range(n):
         mp[t % 2, t // 2 : t // 2 + 1, :] = jnp.sum(
             colacc[order_ref[0, t]], axis=0, keepdims=True
         )
-    mass_sent = []
     for d in range(1, n):
         to = seq_peer(d)
-        copy = copy_to(mp.at[to % 2], mr.at[me], msem, (d,), {"seq": to})
-        copy.start()
-        mass_sent.append(copy)
+        copy_to(mp.at[to % 2], mr.at[me], msem, (), {"seq": to}).start()
     mr[me] = mp[core]
 
-    for copy in queries_passed:
-        copy.wait_recv()
-    for copy in values_sent:
-        copy.wait_recv()
+    waits["query_near"].wait_recv()
+    waits["value"].wait_recv()
 
     def turn_features(s, carry):
         ft[at(core, head), at(s, rows)] = qg[2 * s + core].T
@@ -414,12 +428,8 @@
     lax.fori_loop(0, chips, turn_features, 0)
     ft[pl.ds(2 * head, vpart), :] = kt[at(chip % 2, vpart), :]
 
-    for copy in preds_sent:
-        copy.wait_recv()
-    for r in range(ROUNDS):
-        stage5(r)
-    for copy in mass_sent:
-        copy.wait_recv()
+    waits["pred"].wait_recv()
+    waits["mass"].wait_recv()
     per_group = n // heads
     labels = []
     for g in range(heads):
@@ -434,18 +444,20 @@
         resid = ((predg[s] - label) * live_row * norm).astype(BF16).astype(F32)
         rs[s] = jnp.concatenate([resid, jnp.zeros_like(resid)], axis=0)
 
+    per_round = CLASSES // ROUNDS
+
     def delta_round(r):
-        base = r * classes
+        base = r * per_round
 
         def tokens(s, carry):
             back = jnp.dot(
                 rs[s].T.astype(BF16),
-                wt[:, base * rows : (base + classes) * rows],
+                wt[:, base * lanes : (base + per_round) * lanes],
                 preferred_element_type=F32,
             )
-            for j in range(classes):
+            for j in range(per_round):
                 held = dq[base + j, at(s, rows), :].astype(jnp.int32).astype(F32)
-                value = back[:, j * rows : (j + 1) * rows] * (held * (1.0 / FIXED) + 0.5)
+                value = back[:, j * lanes : (j + 1) * lanes] * (held * (1.0 / FIXED) + 0.5)
                 dg[base + j, at(s, rows), :] = value.astype(BF16)
             return carry
 
@@ -457,17 +469,16 @@
 
     def term(r, which):
         lhs = ft[at(which, half), :]
-        parts = []
-        for j in range(0, classes, 2):
-            rhs = jnp.concatenate([dg[r * classes + j], dg[r * classes + j + 1]], axis=1)
-            parts.append(jnp.dot(lhs, rhs, preferred_element_type=F32))
+        parts = [
+            jnp.dot(lhs, dg[r * per_round + j], preferred_element_type=F32)
+            for j in range(per_round)
+        ]
         return jnp.concatenate(parts, axis=1)
 
     def start_of(target):
         return lax.rem(share_rows * target + 2 * SIDE * chip, half // GRAN)
 
     swaps = []
-    spread = []
 
     def swap(r):
         cs[r] = term(r, 1 - core)
@@ -485,13 +496,12 @@
             to = batch_peer(d)
             copy = copy_to(
                 sb.at[r, pl.ds(start_of(to), share_rows)],
-                xr.at[r, d],
+                xr.at[r, d - 1],
                 xsem,
-                (r, d),
+                (r,),
                 {"batch": to},
             )
             copy.start()
-            spread.append((r, copy))
 
     def granule(i):
         q_gran = 2 * head // GRAN
@@ -537,10 +547,8 @@
 
     def finish(r):
         value = sb[r, pl.ds(start_of(mb), share_rows)]
-        for which, copy in spread:
-            if which == r:
-                copy.wait_recv()
-        for d in range(1, nb):
+        waiter(xr.at[r], xsem, (r,)).wait_recv()
+        for d in range(nb - 1):
             value = value + xr[r, d]
         fin[r] = value
         for e in range(share_rows):
@@ -554,64 +562,81 @@
             def _(r=r, e=e):
                 fout[r, e] = fin[r, e]
 
-    delta_round(0)
-    swap(0)
+    every = n // otc.shape[0]
+    pieces = otc.shape[0]
+    reduces = lax.rem(me, every) == 0
     resid32 = rs[chip]
-    out_term = jnp.dot(resid32.astype(BF16), act[...], preferred_element_type=F32)
-    width = hidden // n
-    bias_sum = jnp.broadcast_to(jnp.sum(resid32[:heads], axis=1, keepdims=True), (heads, width))
+    out_term = jnp.dot(resid32.astype(BF16), act[...], preferred_element_type=F32)[:heads]
+    lane_row = lax.broadcasted_iota(jnp.int32, (heads, rows), 1)
+    bias_row = jnp.sum(
+        jnp.where(
+            lane_row == group_index, jnp.sum(resid32[:heads], axis=1, keepdims=True), 0.0
+        ),
+        axis=0,
+        keepdims=True,
+    )
     delta = (
         jnp.dot(resid32.T.astype(BF16), wt, preferred_element_type=F32) * slope[...]
     ).astype(BF16)
     delta_sum = jnp.sum(delta.astype(F32), axis=0, keepdims=True)
-    for p in range(n):
-        otc[p, :heads] = out_term[:heads, p * width : (p + 1) * width]
-        otc[p, heads : 2 * heads] = bias_sum
-        otc[p, 2 * heads :] = jnp.broadcast_to(
-            delta_sum[:, p * width : (p + 1) * width], (heads, width)
-        )
-    first = []
-    for d in range(1, n):
-        to = seq_peer(d)
-        copy = copy_to(otc.at[to], otr.at[d], osem, (d,), {"seq": to})
-        copy.start()
-        first.append(copy)
+    filler = jnp.zeros((heads - 2, rows), F32)
+    for p in range(pieces):
+        span = slice(p * rows, (p + 1) * rows)
+        otc[p] = jnp.concatenate([out_term[:, span], delta_sum[:, span], bias_row, filler], axis=0)
+
+    def small_copy(p):
+        return copy_to(otc.at[p], otr.at[me], osem, (), {"seq": jnp.int32(p * every)})
+
+    for p in range(pieces):
+
+        @pl.when(me != p * every)
+        def _(p=p):
+            small_copy(p).start()
+
+    stage5()
+    delta_round(0)
+    swap(0)
+
+    @pl.when(reduces)
+    def _():
+        otr[me] = otc[me // every]
+        waiter(otr.at[pl.ds(0, n - 1)], osem, ()).wait_recv()
+        total = otr[0]
+        for d in range(1, n):
+            total = total + otr[d]
+        obs[...] = total
+        for d in range(1, nb):
+            copy_to(obs, obr.at[d - 1], bsem, (), {"batch": batch_peer(d)}).start()
+
     reduce_chip(0)
     delta_round(1)
     swap(1)
-    small = otc[me]
-    for d in range(1, n):
-        first[d - 1].wait_recv()
-        small = small + otr[d]
-    obs[...] = small
-    second = []
-    for d in range(1, nb):
-        copy = copy_to(obs, obr.at[d], bsem, (d,), {"batch": batch_peer(d)})
-        copy.start()
-        second.append(copy)
+
+    @pl.when(reduces)
+    def _():
+        waiter(obr, bsem, ()).wait_recv()
+        total = obs[...]
+        for d in range(nb - 1):
+            total = total + obr[d]
+        ofin[me // every] = total
+        done = ofin.at[me // every]
+        for d in range(1, n):
+            copy_to(done, done, hsem, (), {"seq": seq_peer(d)}).start()
+
     reduce_chip(1)
     finish(0)
-    small = obs[...]
-    for d in range(1, nb):
-        second[d - 1].wait_recv()
-        small = small + obr[d]
-    ofin[me] = small
-    third = []
-    for d in range(1, n):
-        copy = copy_to(ofin.at[me], ofin.at[me], hsem, (d,), {"seq": seq_peer(d)})
-        copy.start()
-        third.append(copy)
     finish(1)
-    for copy in third:
-        copy.wait_recv()
-    small_ref[:heads] = jnp.concatenate([ofin[p, :heads] for p in range(n)], axis=1)
-    gb = jnp.concatenate([ofin[p, 2 * heads : 2 * heads + 1] for p in range(n)], axis=1)
-    column = ofin[0, heads : 2 * heads, :1]
-    lane_all = lax.broadcasted_iota(jnp.int32, (heads, hidden), 1)
-    ob = jnp.sum(jnp.where(lane_all == group_index, column, 0.0), axis=0, keepdims=True)
-    small_ref[heads:] = jnp.concatenate(
-        [gb, ob, jnp.zeros((heads - 2, hidden), F32)], axis=0
-    )
+
+    @pl.when(reduces)
+    def _():
+        waiter(ofin.at[pl.ds(0, pieces - 1)], hsem, ()).wait_recv()
+
+    @pl.when(jnp.logical_not(reduces))
+    def _():
+        waiter(ofin, hsem, ()).wait_recv()
+
+    small = jnp.concatenate([ofin[p] for p in range(pieces)], axis=1)
+    small_ref[...] = small
     for r in range(ROUNDS):
         for e in range(share_rows):
 
@@ -620,22 +645,23 @@
                 final_copy(r, e).wait_recv()
 
             grad_ref[e * GRAN : (e + 1) * GRAN, r * piece : (r + 1) * piece] = fout[r, e]
-    for copy in (
-        key_far
-        + key_near
-        + queries_sent
-        + queries_passed
-        + values_sent
-        + mass_sent
-        + preds_sent
-        + list(gathered.values())
-        + first
-        + second
-        + third
-        + swaps
-        + [copy for _, copy in spread]
-    ):
-        copy.wait_send()
+    for wait in waits.values():
+        wait.wait_send()
+    gathered(dq.at[:, pl.ds(0, (SIDE * SIDE - 1) * rows)], 0, 0).wait_send()
+
+    @pl.when(reduces)
+    def _():
+        waiter(otc.at[pl.ds(0, pieces - 1)], osem, ()).wait_send()
+        waiter(obr, bsem, ()).wait_send()
+        waiter(otr.at[pl.ds(0, n - 1)], hsem, ()).wait_send()
+
+    @pl.when(jnp.logical_not(reduces))
+    def _():
+        waiter(otc, osem, ()).wait_send()
+
+    for r in range(ROUNDS):
+        swaps[r].wait_send()
+        waiter(xr.at[r], xsem, (r,)).wait_send()
     for r in range(ROUNDS):
         for e in range(share_rows):
 
@@ -669,7 +695,6 @@
     total = n * rows
     chips = n // 2
     part = feat // n // nb
-    width = hidden // n
     chip_feat = feat // chips
     piece = hidden // ROUNDS
     grans = chip_feat // 2 // GRAN
@@ -703,34 +728,34 @@
             pltpu.VMEM((n, chips, rows), F32),
             pltpu.VMEM((chips, heads, rows), F32),
             pltpu.VMEM((chips, 2 * heads, rows), F32),
-            pltpu.VMEM((hidden // rows, total // 2, rows), jnp.int16),
-            pltpu.VMEM((hidden // rows, total // 2, rows), BF16),
-            pltpu.VMEM((n, 3 * heads, width), F32),
-            pltpu.VMEM((n, 3 * heads, width), F32),
-            pltpu.VMEM((3 * heads, width), F32),
-            pltpu.VMEM((nb, 3 * heads, width), F32),
-            pltpu.VMEM((n, 3 * heads, width), F32),
+            pltpu.VMEM((CLASSES, total // 2, hidden // CLASSES), jnp.int16),
+            pltpu.VMEM((CLASSES, total // 2, hidden // CLASSES), BF16),
+            pltpu.VMEM((hidden // rows, 2 * heads, rows), F32),
+            pltpu.VMEM((n, 2 * heads, rows), F32),
+            pltpu.VMEM((2 * heads, rows), F32),
+            pltpu.VMEM((nb - 1, 2 * heads, rows), F32),
+            pltpu.VMEM((hidden // rows, 2 * heads, rows), F32),
             pltpu.VMEM((ROUNDS, chip_feat // 2, piece), F32),
             pltpu.VMEM((ROUNDS, chip_feat // 2, piece), F32),
             pltpu.VMEM((ROUNDS, grans + share_rows - 1, GRAN, piece), F32),
-            pltpu.VMEM((ROUNDS, nb, share_rows, GRAN, piece), F32),
+            pltpu.VMEM((ROUNDS, nb - 1, share_rows, GRAN, piece), F32),
             pltpu.VMEM((ROUNDS, share_rows, GRAN, piece), F32),
             pltpu.VMEM((ROUNDS, share_rows, GRAN, piece), F32),
             pltpu.SMEM((n,), jnp.int32),
             dma,
-            dma((2, n)),
-            dma((2, chips)),
-            dma((2, chips)),
-            dma((2, chips)),
-            dma((2, chips)),
-            dma((2, n)),
-            dma((2, chips)),
-            dma((2, ROUNDS, hidden // rows // ROUNDS, SIDE * SIDE)),
-            dma((2, n)),
-            dma((2, nb)),
-            dma((2, n)),
+            dma((2,)),
+            dma((2,)),
+            dma((2,)),
+            dma((2,)),
+            dma((2,)),
+            dma((2,)),
+            dma((2,)),
+            dma((CLASSES + 1, SIDE + 4)),
+            dma((2,)),
+            dma((2,)),
+            dma((2,)),
             dma((2, ROUNDS)),
-            dma((2, ROUNDS, nb)),
+            dma((2, ROUNDS)),
             dma((2, ROUNDS, share_rows)),
         ],
         compiler_params=pltpu.CompilerParams(

time: 99 us -> 90.5 us (0.914)
  Pallas kernels: 96.7 us -> 89 us
    pallas_call x1, Pallas kernels: 95 us -> 87.4 us  [on_device(): pl.pallas_call(functools.partial(kernel, n, nb, norm, scale), out_shape=(...]
where the time goes in v3:
time: 90.5 us; the launch traced here: 90.3 us
  Pallas kernels  89 us (98%)
  between operations  1.29 us (1%)
    pallas_call x1, Pallas kernels, on_device(): pl.pallas_call(functools.partial(kernel, n, nb, norm, scale), out_shape=(...  87.4 us

profile of v3, /device:TPU:8, one launch (start us, length us, event | category | flops | bytes accessed | tf_op | source)
XLA Modules:
  0.0 90.3 jit_solution(2919612426311307703)
XLA Ops:
  1.3 87.4 %shard_map.120 = (f32[48,1024]{1,0:T(8,128)}, f32[16,1024]{1,0:T(8,128)}) custom-call(bf16[128,4096]{1,0:T(8,128)(2,1)} %bitcast.9, bf16[128,1024]{1,0:T(8,128)(2,1)} %bitcast.10, bf16[128,1024]{1,0:T(8,128)(2,1)} %bitcast.11, bf16[6144,1024]{1,0:T(8,128)(2,1)} %w_ref.1, f32[1,1024]{1,0:T(1,128)} %bitcast.13, bf16[8,1024]{1,0:T(8,128)(2,1)} %bitcast.12, ...), custom_call_target="tpu_custom_call" | custom-call | tf_op jit(solution)/shard_map/pallas_call | solution.py:703
  88.7 1.6 %shard_map.121 = (f32[48,1024]{1,0:T(8,128)}, f32[8,1024]{1,0:T(8,128)}, f32[1,1024]{1,0:T(1,128)}, f32[1,8]{1,0:T(1,128)}) custom-call(f32[48,1024]{1,0:T(8,128)} %get-tuple-element.10.grad_in, f32[16,1024]{1,0:T(8,128)} %get-tuple-element.11.small_in), custom_call_target="tpu_custom_call" | custom-call | tf_op jit(solution)/shard_map/pallas_call | solution.py:775

commit v4 on v3

--- a/solution.py
+++ b/solution.py
@@ -12,7 +12,7 @@
 BF16 = jnp.bfloat16
 MESH = pl.DeviceIdType.MESH
 SIDE = 4
-ROUNDS = 2
+ROUNDS = 4
 CLASSES = 4
 FIXED = 54000.0
 GRAN = 16
@@ -73,6 +73,7 @@
     mr,
     predg,
     rs,
+    rt,
     dq,
     dg,
     otc,
@@ -163,16 +164,6 @@
         copy.start()
     vpart = kd // chips
     value_base = 2 * head + vpart
-    for d in range(1, chips):
-        to = chip_peer(d)
-        copy = copy_to(
-            vt.at[at(to, vpart)],
-            ft.at[pl.ds(value_base, vpart), at(chip, rows)],
-            vsem,
-            (),
-            {"seq": to * 2 + core},
-        )
-        copy.start()
     qg[me] = q_ref[:, at(me, head)]
     qo[at(chip, rows), :] = q_ref[:, at(pair, head)]
     kg[me] = k_ref[:, at(chip // 2, head)]
@@ -352,18 +343,19 @@
         ks[at(p, rows), :] = kg[inv[p]]
         return carry
 
-    lax.fori_loop(0, n, sort_keys, 0)
+    lax.fori_loop(0, n, sort_keys, 0, unroll=8)
     colacc[...] = jnp.zeros_like(colacc)
     step = 4
     wide = step * rows
-    row_index = lax.broadcasted_iota(jnp.int32, (rows, 1), 0)
+    tall = 2 * rows
+    row_index = lax.broadcasted_iota(jnp.int32, (tall, 1), 0)
     lane_wide = lax.broadcasted_iota(jnp.int32, (1, wide), 1)
 
     for w in range(n // step):
 
         def query_block(t, carry, w=w):
-            block = w * step + t
-            queries = qg[inv[block]]
+            block = w * step + 2 * t
+            queries = jnp.concatenate([qg[inv[block]], qg[inv[block + 1]]], axis=0)
             best = None
             for kc in range(w + 1):
                 score = lax.dot_general(
@@ -373,7 +365,7 @@
                     preferred_element_type=F32,
                 )
                 if kc == w:
-                    score = jnp.where(lane_wide <= row_index + t * rows, score, -1e30)
+                    score = jnp.where(lane_wide <= row_index + t * tall, score, -1e30)
                 sref[:, kc * wide : (kc + 1) * wide] = score
                 for j in range(step):
                     part = score[:, j * rows : (j + 1) * rows]
@@ -391,21 +383,19 @@
             for kb in range((w + 1) * step):
                 span = slice(kb * rows, (kb + 1) * rows)
                 part = sref[:, span] * share
-                colacc[kb] += jnp.sum(part.reshape(rows // 8, 8, rows), axis=0)
+                colacc[kb] += jnp.sum(part.reshape(tall // 8, 8, rows), axis=0)
             return carry
 
         if w == n // step - 1:
-            lax.fori_loop(0, step // 2, query_block, 0)
-            stage4()
-            lax.fori_loop(step // 2, step, query_block, 0)
+            lax.fori_loop(0, 1, query_block, 0)
+            stage3()
+            lax.fori_loop(1, 2, query_block, 0)
         else:
-            lax.fori_loop(0, step, query_block, 0)
-        if w == 2:
+            lax.fori_loop(0, 2, query_block, 0)
+        if w == 3:
             stage1()
-        elif w == 4:
+        elif w == 5:
             stage2()
-        elif w == 6:
-            stage3()
 
     for t in range(n):
         mp[t % 2, t // 2 : t // 2 + 1, :] = jnp.sum(
@@ -417,7 +407,6 @@
     mr[me] = mp[core]
 
     waits["query_near"].wait_recv()
-    waits["value"].wait_recv()
 
     def turn_features(s, carry):
         ft[at(core, head), at(s, rows)] = qg[2 * s + core].T
@@ -425,8 +414,19 @@
         kt[:, at(s, rows)] = kg[2 * s + core].T
         return carry
 
-    lax.fori_loop(0, chips, turn_features, 0)
+    lax.fori_loop(0, chips, turn_features, 0, unroll=4)
     ft[pl.ds(2 * head, vpart), :] = kt[at(chip % 2, vpart), :]
+    stage4()
+    for d in range(1, chips):
+        to = chip_peer(d)
+        copy = copy_to(
+            vt.at[at(to, vpart)],
+            ft.at[pl.ds(value_base, vpart), at(chip, rows)],
+            vsem,
+            (),
+            {"seq": to * 2 + core},
+        )
+        copy.start()
 
     waits["pred"].wait_recv()
     waits["mass"].wait_recv()
@@ -442,26 +442,30 @@
         label = jnp.concatenate([part[s : s + 1] for part in labels], axis=0)
         live_row = (lane + order_ref[0, 2 * s + core] * rows < limit).astype(F32)
         resid = ((predg[s] - label) * live_row * norm).astype(BF16).astype(F32)
-        rs[s] = jnp.concatenate([resid, jnp.zeros_like(resid)], axis=0)
+        resid = jnp.concatenate([resid, jnp.zeros_like(resid)], axis=0)
+        rs[s] = resid
+        rt[s * rows : (s + 1) * rows, :] = resid.T.astype(BF16)
 
     per_round = CLASSES // ROUNDS
 
     def delta_round(r):
         base = r * per_round
 
+        many = 4 * rows
+
         def tokens(s, carry):
             back = jnp.dot(
-                rs[s].T.astype(BF16),
+                rt[at(s, many), :],
                 wt[:, base * lanes : (base + per_round) * lanes],
                 preferred_element_type=F32,
             )
             for j in range(per_round):
-                held = dq[base + j, at(s, rows), :].astype(jnp.int32).astype(F32)
+                held = dq[base + j, at(s, many), :].astype(jnp.int32).astype(F32)
                 value = back[:, j * lanes : (j + 1) * lanes] * (held * (1.0 / FIXED) + 0.5)
-                dg[base + j, at(s, rows), :] = value.astype(BF16)
+                dg[base + j, at(s, many), :] = value.astype(BF16)
             return carry
 
-        lax.fori_loop(0, chips, tokens, 0)
+        lax.fori_loop(0, chips // 4, tokens, 0)
 
     half = ft.shape[0] // 2
     piece = hidden // ROUNDS
@@ -543,7 +547,7 @@
         return which * 2 + jnp.where(i >= half // GRAN, 1, 0)
 
     def final_copy(r, e):
-        return copy_to(fin.at[r, e], fout.at[r, e], gsem, (r, e), {"seq": owner_of(e)})
+        return copy_to(fin.at[r, e], fout.at[r, e], gsem, (e,), {"seq": owner_of(e)})
 
     def finish(r):
         value = sb[r, pl.ds(start_of(mb), share_rows)]
@@ -595,37 +599,44 @@
 
     stage5()
     delta_round(0)
+    waits["value"].wait_recv()
     swap(0)
 
-    @pl.when(reduces)
-    def _():
-        otr[me] = otc[me // every]
-        waiter(otr.at[pl.ds(0, n - 1)], osem, ()).wait_recv()
-        total = otr[0]
-        for d in range(1, n):
-            total = total + otr[d]
-        obs[...] = total
-        for d in range(1, nb):
-            copy_to(obs, obr.at[d - 1], bsem, (), {"batch": batch_peer(d)}).start()
-
-    reduce_chip(0)
-    delta_round(1)
-    swap(1)
-
-    @pl.when(reduces)
-    def _():
-        waiter(obr, bsem, ()).wait_recv()
-        total = obs[...]
-        for d in range(nb - 1):
-            total = total + obr[d]
-        ofin[me // every] = total
-        done = ofin.at[me // every]
-        for d in range(1, n):
-            copy_to(done, done, hsem, (), {"seq": seq_peer(d)}).start()
-
-    reduce_chip(1)
-    finish(0)
-    finish(1)
+    def small_over_seq():
+        @pl.when(reduces)
+        def _():
+            otr[me] = otc[me // every]
+            waiter(otr.at[pl.ds(0, n - 1)], osem, ()).wait_recv()
+            total = otr[0]
+            for d in range(1, n):
+                total = total + otr[d]
+            obs[...] = total
+            for d in range(1, nb):
+                copy_to(obs, obr.at[d - 1], bsem, (), {"batch": batch_peer(d)}).start()
+
+    def small_over_batch():
+        @pl.when(reduces)
+        def _():
+            waiter(obr, bsem, ()).wait_recv()
+            total = obs[...]
+            for d in range(nb - 1):
+                total = total + obr[d]
+            ofin[me // every] = total
+            done = ofin.at[me // every]
+            for d in range(1, n):
+                copy_to(done, done, hsem, (), {"seq": seq_peer(d)}).start()
+
+    for r in range(1, ROUNDS):
+        delta_round(r)
+        swap(r)
+        reduce_chip(r - 1)
+        if r == ROUNDS // 2:
+            small_over_seq()
+    reduce_chip(ROUNDS - 1)
+    for r in range(ROUNDS):
+        finish(r)
+        if r == 1:
+            small_over_batch()
 
     @pl.when(reduces)
     def _():
@@ -637,13 +648,13 @@
 
     small = jnp.concatenate([ofin[p] for p in range(pieces)], axis=1)
     small_ref[...] = small
-    for r in range(ROUNDS):
-        for e in range(share_rows):
-
-            @pl.when(maker_of(e) != me)
-            def _(r=r, e=e):
-                final_copy(r, e).wait_recv()
-
+    for e in range(share_rows):
+
+        @pl.when(maker_of(e) != me)
+        def _(e=e):
+            waiter(fout.at[:, e], gsem, (e,)).wait_recv()
+
+        for r in range(ROUNDS):
             grad_ref[e * GRAN : (e + 1) * GRAN, r * piece : (r + 1) * piece] = fout[r, e]
     for wait in waits.values():
         wait.wait_send()
@@ -662,12 +673,11 @@
     for r in range(ROUNDS):
         swaps[r].wait_send()
         waiter(xr.at[r], xsem, (r,)).wait_send()
-    for r in range(ROUNDS):
-        for e in range(share_rows):
-
-            @pl.when(owner_of(e) != me)
-            def _(r=r, e=e):
-                final_copy(r, e).wait_send()
+    for e in range(share_rows):
+
+        @pl.when(owner_of(e) != me)
+        def _(e=e):
+            waiter(fin.at[:, e], gsem, (e,)).wait_send()
 
 
 def emit(grad_in, small_in, grad_ref, gw_ref, gb_ref, ob_ref):
@@ -722,12 +732,13 @@
             pltpu.VMEM((kd, rows), BF16),
             pltpu.VMEM((rows, hidden), F32),
             pltpu.VMEM((rows, hidden), BF16),
-            pltpu.VMEM((rows, total), F32),
+            pltpu.VMEM((2 * rows, total), F32),
             pltpu.VMEM((n, 8, rows), F32),
             pltpu.VMEM((2, chips, rows), F32),
             pltpu.VMEM((n, chips, rows), F32),
             pltpu.VMEM((chips, heads, rows), F32),
             pltpu.VMEM((chips, 2 * heads, rows), F32),
+            pltpu.VMEM((total // 2, 2 * heads), BF16),
             pltpu.VMEM((CLASSES, total // 2, hidden // CLASSES), jnp.int16),
             pltpu.VMEM((CLASSES, total // 2, hidden // CLASSES), BF16),
             pltpu.VMEM((hidden // rows, 2 * heads, rows), F32),
@@ -756,7 +767,7 @@
             dma((2,)),
             dma((2, ROUNDS)),
             dma((2, ROUNDS)),
-            dma((2, ROUNDS, share_rows)),
+            dma((2, share_rows)),
         ],
         compiler_params=pltpu.CompilerParams(
             collective_id=0, has_side_effects=True, vmem_limit_bytes=60 * 1024 * 1024

time: 90.5 us -> 84.3 us (0.931)
  Pallas kernels: 89 us -> 82.9 us
    pallas_call x1, Pallas kernels: 87.4 us -> 81.3 us  [on_device(): pl.pallas_call(functools.partial(kernel, n, nb, norm, scale), out_shape=(...]
where the time goes in v4:
time: 84.3 us; the launch traced here: 84.2 us
  Pallas kernels  82.9 us (98%)
  between operations  1.29 us (2%)
    pallas_call x1, Pallas kernels, on_device(): pl.pallas_call(functools.partial(kernel, n, nb, norm, scale), out_shape=(...  81.3 us

profile of v4, /device:TPU:8, one launch (start us, length us, event | category | flops | bytes accessed | tf_op | source)
XLA Modules:
  0.0 84.2 jit_solution(3450902782685316902)
XLA Ops:
  1.3 81.3 %shard_map.120 = (f32[48,1024]{1,0:T(8,128)}, f32[16,1024]{1,0:T(8,128)}) custom-call(bf16[128,4096]{1,0:T(8,128)(2,1)} %bitcast.9, bf16[128,1024]{1,0:T(8,128)(2,1)} %bitcast.10, bf16[128,1024]{1,0:T(8,128)(2,1)} %bitcast.11, bf16[6144,1024]{1,0:T(8,128)(2,1)} %w_ref.1, f32[1,1024]{1,0:T(1,128)} %bitcast.13, bf16[8,1024]{1,0:T(8,128)(2,1)} %bitcast.12, ...), custom_call_target="tpu_custom_call" | custom-call | tf_op jit(solution)/shard_map/pallas_call | solution.py:713
  82.5 1.6 %shard_map.121 = (f32[48,1024]{1,0:T(8,128)}, f32[8,1024]{1,0:T(8,128)}, f32[1,1024]{1,0:T(1,128)}, f32[1,8]{1,0:T(1,128)}) custom-call(f32[48,1024]{1,0:T(8,128)} %get-tuple-element.10.grad_in, f32[16,1024]{1,0:T(8,128)} %get-tuple-element.11.small_in), custom_call_target="tpu_custom_call" | custom-call | tf_op jit(solution)/shard_map/pallas_call | solution.py:786

commit v5 on v4

--- a/solution.py
+++ b/solution.py
@@ -566,6 +566,10 @@
             def _(r=r, e=e):
                 fout[r, e] = fin[r, e]
 
+    stage5()
+    delta_round(0)
+    waits["value"].wait_recv()
+    swap(0)
     every = n // otc.shape[0]
     pieces = otc.shape[0]
     reduces = lax.rem(me, every) == 0
@@ -597,10 +601,6 @@
         def _(p=p):
             small_copy(p).start()
 
-    stage5()
-    delta_round(0)
-    waits["value"].wait_recv()
-    swap(0)
 
     def small_over_seq():
         @pl.when(reduces)

time: 84.3 us -> 84 us (level)
  no operation moved by 1% of the time
where the time goes in v5:
time: 84 us; the launch traced here: 83.8 us
  Pallas kernels  82.6 us (98%)
  between operations  1.29 us (2%)
    pallas_call x1, Pallas kernels, on_device(): pl.pallas_call(functools.partial(kernel, n, nb, norm, scale), out_shape=(...  80.9 us

profile of v5, /device:TPU:8, one launch (start us, length us, event | category | flops | bytes accessed | tf_op | source)
XLA Modules:
  0.0 83.8 jit_solution(4575148120029761465)
XLA Ops:
  1.3 80.9 %shard_map.120 = (f32[48,1024]{1,0:T(8,128)}, f32[16,1024]{1,0:T(8,128)}) custom-call(bf16[128,4096]{1,0:T(8,128)(2,1)} %bitcast.9, bf16[128,1024]{1,0:T(8,128)(2,1)} %bitcast.10, bf16[128,1024]{1,0:T(8,128)(2,1)} %bitcast.11, bf16[6144,1024]{1,0:T(8,128)(2,1)} %w_ref.1, f32[1,1024]{1,0:T(1,128)} %bitcast.13, bf16[8,1024]{1,0:T(8,128)(2,1)} %bitcast.12, ...), custom_call_target="tpu_custom_call" | custom-call | tf_op jit(solution)/shard_map/pallas_call | solution.py:713
  82.2 1.6 %shard_map.121 = (f32[48,1024]{1,0:T(8,128)}, f32[8,1024]{1,0:T(8,128)}, f32[1,1024]{1,0:T(1,128)}, f32[1,8]{1,0:T(1,128)}) custom-call(f32[48,1024]{1,0:T(8,128)} %get-tuple-element.10.grad_in, f32[16,1024]{1,0:T(8,128)} %get-tuple-element.11.small_in), custom_call_target="tpu_custom_call" | custom-call | tf_op jit(solution)/shard_map/pallas_call | solution.py:786
